TPU v7x, 128 devices: a whole 4x4x4 slice. The times are simulated.
128 devices in a mesh: leaf: 16 (over x, z), rows: 8 (over y, core).
Axes of the slice: x: 4, y: 4, z: 4, core: 2. Of those that a mesh axis runs over, the one named last changes fastest.
Arguments:
- loads_first: bfloat16 [98304, 256], P(('leaf', 'rows')), may hold values from -6 to 6
- loads_second: bfloat16 [49152, 256], P(('leaf', 'rows')), may hold values from -6 to 6
- loads_third: bfloat16 [24576, 256], P(('leaf', 'rows')), may hold values from -6 to 6
- loads_fourth: bfloat16 [12288, 256], P(('leaf', 'rows')), may hold values from -6 to 6
- inverse_first: bfloat16 [98304, 6144], P(('leaf', 'rows')), as said below
- inverse_second: bfloat16 [49152, 6144], P(('leaf', 'rows')), as said below
- inverse_third: bfloat16 [24576, 6144], P(('leaf', 'rows')), as said below
- inverse_fourth: bfloat16 [12288, 6144], P(('leaf', 'rows')), as said below
- panel_first: bfloat16 [1536, 98304], P(None, ('leaf', 'rows')), may hold values from -0.078125 to 0.078125
- panel_second: bfloat16 [1536, 49152], P(None, ('leaf', 'rows')), may hold values from -0.078125 to 0.078125
- panel_third: bfloat16 [1536, 24576], P(None, ('leaf', 'rows')), may hold values from -0.078125 to 0.078125
- panel_fourth: bfloat16 [1536, 12288], P(None, ('leaf', 'rows')), may hold values from -0.078125 to 0.078125
- blocks_first: int32 [16, 12], replicated, may hold values from 0 to 47, as said below
- blocks_second: int32 [8, 12], replicated, may hold values from 0 to 47, as said below
- blocks_third: int32 [4, 12], replicated, may hold values from 0 to 47, as said below
Outputs:
- solved_first: bfloat16 [98304, 256], P(('leaf', 'rows'))
- solved_second: bfloat16 [49152, 256], P(('leaf', 'rows'))
- solved_third: bfloat16 [24576, 256], P(('leaf', 'rows'))
- solved_fourth: bfloat16 [12288, 256], P(('leaf', 'rows'))
- ancestor_update: float32 [3072, 256], P(('leaf', 'rows'))
Inputs may be any that keep to these rules, and one draw needn't show every extreme that they name: `blocks_first`: each row lists 12 distinct block numbers in increasing order. `blocks_second`: each row lists 12 distinct block numbers in increasing order. `blocks_third`: each row lists 12 distinct block numbers in increasing order. `inverse_first`: each block of 6144 rows is lower triangular with a positive diagonal. `inverse_second`: each block of 6144 rows is lower triangular with a positive diagonal. `inverse_third`: each block of 6144 rows is lower triangular with a positive diagonal. `inverse_fourth`: each block of 6144 rows is lower triangular with a positive diagonal.
All inputs are finite; a program needn't handle non-finite values.
Results may differ from a plain program's by a relative error of at most 0.015.
Values may be sent and summed in bfloat16 or wider, within the bound.
A program may use at most 128 MiB of HBM per device.

v0:
```python
import jax
import jax.numpy as jnp
from jax import lax
from jax.sharding import PartitionSpec as P

S = 6144
BLK = 128


def partner_2(value, axis, apart):
    return lax.ppermute(value, axis, [(i, i ^ 1 << apart) for i in range(lax.axis_size(axis))])


def stack_group(local_rows, level_index):
    gathered = lax.all_gather(local_rows, "rows", axis=0, tiled=True)
    leaf_index = lax.axis_index("leaf")
    for bit_number in range(level_index):
        partner = partner_2(gathered, "leaf", bit_number)
        is_upper = leaf_index >> bit_number & 1 == 1
        lower_part = jnp.where(is_upper, partner, gathered)
        upper_part = jnp.where(is_upper, gathered, partner)
        gathered = jnp.concatenate([lower_part, upper_part], 0)
    return gathered


def reduce_whole(partial_value, level_index, sibling):
    summed = lax.psum(partial_value, "rows")
    for bit_number in range(level_index):
        summed = summed + partner_2(summed.astype(jnp.bfloat16), "leaf", bit_number).astype(
            summed.dtype
        )
    if sibling:
        return (summed, partner_2(summed, "leaf", level_index))
    return (summed, None)


def place_rows(update, table_row):
    columns = update.shape[1]
    selector = (table_row[:, None] == jnp.arange(S // BLK, dtype=jnp.int32)[None, :]).astype(
        jnp.float32
    )
    blocks = update.reshape(table_row.shape[0], BLK, columns)
    spread = jnp.einsum("us,ubn->sbn", selector, blocks, precision=lax.Precision.HIGHEST)
    return spread.reshape(S, columns)


def per_device(
    loads_first,
    loads_second,
    loads_third,
    loads_fourth,
    inverse_first,
    inverse_second,
    inverse_third,
    inverse_fourth,
    panel_first,
    panel_second,
    panel_third,
    panel_fourth,
    blocks_first,
    blocks_second,
    blocks_third,
):
    load_list = [loads_first, loads_second, loads_third, loads_fourth]
    inverse_list = [inverse_first, inverse_second, inverse_third, inverse_fourth]
    panel_list = [panel_first, panel_second, panel_third, panel_fourth]
    table_list = [blocks_first, blocks_second, blocks_third]
    leaf_index = lax.axis_index("leaf")
    own_up = None
    sib_up = None
    solved_list = []
    for level_index in range(4):
        gathered = stack_group(load_list[level_index], level_index)
        if level_index == 0:
            prepared = gathered
        else:
            row_table = table_list[level_index - 1]
            child_index = leaf_index >> level_index - 1
            own_row = lax.dynamic_index_in_dim(row_table, child_index, 0, keepdims=False)
            sib_row = lax.dynamic_index_in_dim(row_table, child_index ^ 1, 0, keepdims=False)
            assembled = (
                gathered.astype(jnp.float32)
                - place_rows(own_up, own_row)
                - place_rows(sib_up, sib_row)
            )
            prepared = assembled.astype(jnp.bfloat16)
        solved = jnp.dot(
            inverse_list[level_index], prepared, preferred_element_type=jnp.float32
        ).astype(jnp.bfloat16)
        solved_list.append(solved)
        partial_value = jnp.dot(panel_list[level_index], solved, preferred_element_type=jnp.float32)
        sibling = level_index < 3
        own_up, sib_up = reduce_whole(partial_value, level_index, sibling)
    row_count = own_up.shape[0] // (8 * lax.axis_size("rows"))
    position = leaf_index % 8 * lax.axis_size("rows") + lax.axis_index("rows")
    ancestor = lax.dynamic_slice_in_dim(own_up, position * row_count, row_count, 0)
    return (solved_list[0], solved_list[1], solved_list[2], solved_list[3], ancestor)


def solution(mesh):
    in_specs = (
        P(("leaf", "rows"), None),
        P(("leaf", "rows"), None),
        P(("leaf", "rows"), None),
        P(("leaf", "rows"), None),
        P(("leaf", "rows"), None),
        P(("leaf", "rows"), None),
        P(("leaf", "rows"), None),
        P(("leaf", "rows"), None),
        P(None, ("leaf", "rows")),
        P(None, ("leaf", "rows")),
        P(None, ("leaf", "rows")),
        P(None, ("leaf", "rows")),
        P(),
        P(),
        P(),
    )
    out_specs = (
        P(("leaf", "rows"), None),
        P(("leaf", "rows"), None),
        P(("leaf", "rows"), None),
        P(("leaf", "rows"), None),
        P(("leaf", "rows"), None),
    )
    return jax.shard_map(
        per_device, mesh=mesh, in_specs=in_specs, out_specs=out_specs, check_vma=False
    )
```

profile of v0, /device:TPU:1, one launch (start us, length us, event | category | flops | bytes accessed | tf_op | source)
XLA Modules:
  0.0 656.0 jit_solution(140681794003926255)
XLA Ops:
  8.7 28.9 %all-gather.5.cloned.1.call-done = bf16[3072,256]{1,0:T(8,128)(2,1)} async-done(((bf16[384,256]{1,0:T(8,128)(2,1)}), bf16[3072,256]{1,0:T(8,128)(2,1)}) %all-gather.5.cloned.1.call-update) | async-done | bytes 1572880 | tf_op jit(solution)/shard_map/all_gather | solution.py:15
  38.9 28.3 %all-gather.3.cloned.1.call-done = bf16[6144,256]{1,0:T(8,128)(2,1)} async-done(((bf16[768,256]{1,0:T(8,128)(2,1)}), bf16[6144,256]{1,0:T(8,128)(2,1)}) %all-gather.3.cloned.1.call-update) | async-done | bytes 3145744 | tf_op jit(solution)/shard_map/all_gather | solution.py:15
  67.2 7.2 %convolution_convert_fusion = bf16[768,256]{1,0:T(8,128)(2,1)S(1)} fusion(bf16[768,6144]{1,0:T(8,128)(2,1)} %param.19, bf16[6144,256]{1,0:T(8,128)(2,1)} %all-gather.3.cloned.1.call-done), kind=kOutput, calls=%fused_computation.38 | convolution fusion | flops 2416115712 | bytes 12976128 | tf_op jit(solution)/shard_map/dot_general | solution.py:87
  77.2 61.8 %all-reduce.5.cloned.1.call-done = f32[1536,256]{0,1:T(8,128)} async-done(((f32[1536,256]{0,1:T(8,128)}), f32[1536,256]{0,1:T(8,128)}) %all-reduce.5.cloned.1.call-update) | async-done | bytes 1572880 | tf_op jit(solution)/shard_map/psum | solution.py:27
  140.3 16.1 %all_gather.14 = bf16[1536,256]{1,0:T(8,128)(2,1)S(1)} all-gather(bf16[192,256]{1,0:T(8,128)(2,1)S(1)} %copy-done.22), channel_id=1, replica_groups=mesh['leaf'=16,'rows'=8] {'rows'}, dimensions={0}, use_global_device_ids=true | all-gather | bytes 884736 | tf_op jit(solution)/shard_map/all_gather | solution.py:15
  166.1 6.3 copy.30
  177.9 4.2 copy.33
  189.5 65.4 %all-reduce.7.cloned.1.call-done = f32[1536,256]{0,1:T(8,128)} async-done(((f32[1536,256]{0,1:T(8,128)}), f32[1536,256]{0,1:T(8,128)}) %all-reduce.7.cloned.1.call-update) | async-done | bytes 1572880 | tf_op jit(solution)/shard_map/psum | solution.py:27
  261.6 11.4 %collective-permute-done.4 = bf16[1536,256]{0,1:T(8,128)(2,1)S(1)} collective-permute-done((bf16[1536,256]{0,1:T(8,128)(2,1)S(1)}, bf16[1536,256]{0,1:T(8,128)(2,1)S(1)}, u32[]{:S(2)}, u32[]{:S(2)}) %collective-permute-start.4) | collective-permute-done | bytes 786464 | tf_op jit(solution)/shard_map/ppermute | solution.py:11
  277.3 19.6 %all_gather.15 = bf16[768,256]{1,0:T(8,128)(2,1)S(1)} all-gather(bf16[96,256]{1,0:T(8,128)(2,1)S(1)} %copy-done.23), channel_id=1, replica_groups=mesh['leaf'=16,'rows'=8] {'rows'}, dimensions={0}, use_global_device_ids=true | all-gather | bytes 442368 | tf_op jit(solution)/shard_map/all_gather | solution.py:15
  298.2 11.0 %collective-permute-done.3 = bf16[3072,256]{1,0:T(8,128)(2,1)} collective-permute-done((bf16[3072,256]{1,0:T(8,128)(2,1)}, bf16[3072,256]{1,0:T(8,128)(2,1)}, u32[]{:S(2)}, u32[]{:S(2)}) %collective-permute-start.3) | collective-permute-done | bytes 1572896 | tf_op jit(solution)/shard_map/ppermute | solution.py:11
  318.1 6.3 copy.36
  324.4 18.5 %collective-permute-done.5 = f32[1536,256]{0,1:T(8,128)} collective-permute-done((f32[1536,256]{0,1:T(8,128)}, f32[1536,256]{0,1:T(8,128)}, u32[]{:S(2)}, u32[]{:S(2)}) %collective-permute-start.5) | collective-permute-done | bytes 1572896 | tf_op jit(solution)/shard_map/ppermute | solution.py:11
  348.1 3.9 copy.39
  358.2 63.2 %all-reduce.9.cloned.1.call-done = f32[1536,256]{0,1:T(8,128)} async-done(((f32[1536,256]{0,1:T(8,128)}), f32[1536,256]{0,1:T(8,128)}) %all-reduce.9.cloned.1.call-update) | async-done | bytes 1572880 | tf_op jit(solution)/shard_map/psum | solution.py:27
  425.7 13.8 %collective-permute-done.9 = bf16[1536,256]{0,1:T(8,128)(2,1)S(1)} collective-permute-done((bf16[1536,256]{0,1:T(8,128)(2,1)S(1)}, bf16[1536,256]{0,1:T(8,128)(2,1)S(1)}, u32[]{:S(2)}, u32[]{:S(2)}) %collective-permute-start.9) | collective-permute-done | bytes 786464 | tf_op jit(solution)/shard_map/ppermute | solution.py:11
  445.1 13.7 %collective-permute-done.10 = bf16[1536,256]{0,1:T(8,128)(2,1)S(1)} collective-permute-done((bf16[1536,256]{0,1:T(8,128)(2,1)S(1)}, bf16[1536,256]{0,1:T(8,128)(2,1)S(1)}, u32[]{:S(2)}, u32[]{:S(2)}) %collective-permute-start.10) | collective-permute-done | bytes 786464 | tf_op jit(solution)/shard_map/ppermute | solution.py:11
  461.9 14.5 %collective-permute-done.8 = bf16[3072,256]{1,0:T(8,128)(2,1)} collective-permute-done((bf16[3072,256]{1,0:T(8,128)(2,1)}, bf16[3072,256]{1,0:T(8,128)(2,1)}, u32[]{:S(2)}, u32[]{:S(2)}) %collective-permute-start.8) | collective-permute-done | bytes 1572896 | tf_op jit(solution)/shard_map/ppermute | solution.py:11
  485.3 6.3 copy.42
  491.6 18.5 %collective-permute-done.11 = f32[1536,256]{0,1:T(8,128)} collective-permute-done((f32[1536,256]{0,1:T(8,128)}, f32[1536,256]{0,1:T(8,128)}, u32[]{:S(2)}, u32[]{:S(2)}) %collective-permute-start.11) | collective-permute-done | bytes 1572896 | tf_op jit(solution)/shard_map/ppermute | solution.py:11
  523.6 68.7 %all-reduce.11.cloned.1.call-done = f32[1536,256]{0,1:T(8,128)} async-done(((f32[1536,256]{0,1:T(8,128)}), f32[1536,256]{0,1:T(8,128)}) %all-reduce.11.cloned.1.call-update) | async-done | bytes 1572880 | tf_op jit(solution)/shard_map/psum | solution.py:27
  595.3 15.2 %collective-permute-done.12 = bf16[1536,256]{0,1:T(8,128)(2,1)S(1)} collective-permute-done((bf16[1536,256]{0,1:T(8,128)(2,1)S(1)}, bf16[1536,256]{0,1:T(8,128)(2,1)S(1)}, u32[]{:S(2)}, u32[]{:S(2)}) %collective-permute-start.12) | collective-permute-done | bytes 786464 | tf_op jit(solution)/shard_map/ppermute | solution.py:11
  613.6 16.2 %collective-permute-done.13 = bf16[1536,256]{0,1:T(8,128)(2,1)S(1)} collective-permute-done((bf16[1536,256]{0,1:T(8,128)(2,1)S(1)}, bf16[1536,256]{0,1:T(8,128)(2,1)S(1)}, u32[]{:S(2)}, u32[]{:S(2)}) %collective-permute-start.13) | collective-permute-done | bytes 786464 | tf_op jit(solution)/shard_map/ppermute | solution.py:11
  633.3 13.8 %collective-permute-done.14 = bf16[1536,256]{0,1:T(8,128)(2,1)} collective-permute-done((bf16[1536,256]{0,1:T(8,128)(2,1)S(1)}, bf16[1536,256]{0,1:T(8,128)(2,1)}, u32[]{:S(2)}, u32[]{:S(2)}) %collective-permute-start.14) | collective-permute-done | bytes 786464 | tf_op jit(solution)/shard_map/ppermute | solution.py:11
  (148 shorter events, 108.3 us)
Async XLA Ops:
  7.2 68.0 %copy-start = (bf16[1536,768]{1,0:T(8,128)(2,1)S(1)}, bf16[1536,768]{1,0:T(8,128)(2,1)}, u32[]{:S(2)}) copy-start(bf16[1536,768]{1,0:T(8,128)(2,1)} %param.23) | copy-start | bytes 7077892
  7.2 30.4 %all-gather.5.cloned.1.call-start = ((), (), s32[]{:S(2)}) async-start(), calls=%async_computation.1 | async-start | bytes 1769472 | tf_op jit(solution)/shard_map/all_gather | solution.py:15
  7.9 59.3 %all-gather.3.cloned.1.call-start = ((), (), s32[]{:S(2)}) async-start(), calls=%async_computation | async-start | bytes 3538944 | tf_op jit(solution)/shard_map/all_gather | solution.py:15
  8.7 130.4 %all-reduce.5.cloned.1.call-start = ((), (), s32[]{:S(2)}) async-start(), calls=%async_computation.2 | async-start | bytes 3145728 | tf_op jit(solution)/shard_map/psum | solution.py:27
  37.6 120.0 %collective-permute-start = (bf16[3072,256]{1,0:T(8,128)(2,1)}, bf16[3072,256]{1,0:T(8,128)(2,1)}, u32[]{:S(2)}, u32[]{:S(2)}) collective-permute-start(bf16[3072,256]{1,0:T(8,128)(2,1)} %all-gather.5.cloned.1.call-done), channel_id=1, source_target_pairs={{0,8},{8,0},{16,24},{24,16},{32,40},{40,32},{48,56},{56,48},{64,72... | collective-permute-start | bytes 4718600 | tf_op jit(solution)/shard_map/ppermute | solution.py:11
  75.1 65.2 %copy-start.22 = (bf16[192,256]{1,0:T(8,128)(2,1)S(1)}, bf16[192,256]{1,0:T(8,128)(2,1)}, u32[]{:S(2)}) copy-start(bf16[192,256]{1,0:T(8,128)(2,1)} %param.17) | copy-start | bytes 294916
  77.2 80.5 %copy-start.12 = (bf16[3072,256]{1,0:T(8,128)(2,1)S(1)}, bf16[3072,256]{1,0:T(8,128)(2,1)}, u32[]{:S(2)}) copy-start(bf16[3072,256]{1,0:T(8,128)(2,1)} %all-gather.5.cloned.1.call-done) | copy-start | bytes 4718596
  77.2 177.8 %all-reduce.7.cloned.1.call-start = ((), (), s32[]{:S(2)}) async-start(), calls=%async_computation.3 | async-start | bytes 3145728 | tf_op jit(solution)/shard_map/psum | solution.py:27
  139.0 33.7 %collective-permute-start.1 = (f32[1536,256]{0,1:T(8,128)}, f32[1536,256]{0,1:T(8,128)}, u32[]{:S(2)}, u32[]{:S(2)}) collective-permute-start(f32[1536,256]{0,1:T(8,128)} %all-reduce.5.cloned.1.call-done), channel_id=1, source_target_pairs={{0,8},{8,0},{16,24},{24,16},{32,40},{40,32},{48,56},{56,48},{64,72... | collective-permute-start | bytes 4718600 | tf_op jit(solution)/shard_map/ppermute | solution.py:11
  156.4 33.0 %collective-permute-start.2 = (bf16[1536,256]{1,0:T(8,128)(2,1)S(1)}, bf16[1536,256]{1,0:T(8,128)(2,1)S(1)}, u32[]{:S(2)}, u32[]{:S(2)}) collective-permute-start(bf16[1536,256]{1,0:T(8,128)(2,1)S(1)} %all_gather.14), channel_id=1, source_target_pairs={{0,8},{8,0},{16,24},{24,16},{32,40},{40,32},{48,56},{56,48},{64,72... | collective-permute-start | bytes 2359304 | tf_op jit(solution)/shard_map/ppermute | solution.py:11
  188.0 233.4 %all-reduce.9.cloned.1.call-start = ((), (), s32[]{:S(2)}) async-start(), calls=%async_computation.4 | async-start | bytes 3145728 | tf_op jit(solution)/shard_map/psum | solution.py:27
  256.4 16.6 %collective-permute-start.4 = (bf16[1536,256]{0,1:T(8,128)(2,1)S(1)}, bf16[1536,256]{0,1:T(8,128)(2,1)S(1)}, u32[]{:S(2)}, u32[]{:S(2)}) collective-permute-start(bf16[1536,256]{0,1:T(8,128)(2,1)S(1)} %convert_element_type.87), channel_id=1, source_target_pairs={{0,8},{8,0},{16,24},{24,16},{32,40},{40,32},{48,56},{56,48},{64,72... | collective-permute-start | bytes 2359304 | tf_op jit(solution)/shard_map/ppermute | solution.py:11
  259.0 50.2 %collective-permute-start.3 = (bf16[3072,256]{1,0:T(8,128)(2,1)}, bf16[3072,256]{1,0:T(8,128)(2,1)}, u32[]{:S(2)}, u32[]{:S(2)}) collective-permute-start(bf16[3072,256]{1,0:T(8,128)(2,1)} %pad_maximum_fusion), channel_id=1, source_target_pairs={{0,16},{8,24},{16,0},{24,8},{32,48},{40,56},{48,32},{56,40},{64,80... | collective-permute-start | bytes 4718600 | tf_op jit(solution)/shard_map/ppermute | solution.py:11
  274.4 68.5 %collective-permute-start.5 = (f32[1536,256]{0,1:T(8,128)}, f32[1536,256]{0,1:T(8,128)}, u32[]{:S(2)}, u32[]{:S(2)}) collective-permute-start(f32[1536,256]{0,1:T(8,128)} %convert_add_fusion.4), channel_id=1, source_target_pairs={{0,16},{8,24},{16,0},{24,8},{32,48},{40,56},{48,32},{56,40},{64,80... | collective-permute-start | bytes 4718600 | tf_op jit(solution)/shard_map/ppermute | solution.py:11
  296.9 59.6 %collective-permute-start.6 = (bf16[768,256]{1,0:T(8,128)(2,1)S(1)}, bf16[768,256]{1,0:T(8,128)(2,1)}, u32[]{:S(2)}, u32[]{:S(2)}) collective-permute-start(bf16[768,256]{1,0:T(8,128)(2,1)S(1)} %all_gather.15), channel_id=1, source_target_pairs={{0,8},{8,0},{16,24},{24,16},{32,40},{40,32},{48,56},{56,48},{64,72... | collective-permute-start | bytes 1179656 | tf_op jit(solution)/shard_map/ppermute | solution.py:11
  356.5 235.8 %all-reduce.11.cloned.1.call-start = ((), (), s32[]{:S(2)}) async-start(), calls=%async_computation.5 | async-start | bytes 3145728 | tf_op jit(solution)/shard_map/psum | solution.py:27
  357.7 66.6 %collective-permute-start.7 = (bf16[1536,256]{1,0:T(8,128)(2,1)S(1)}, bf16[1536,256]{1,0:T(8,128)(2,1)}, u32[]{:S(2)}, u32[]{:S(2)}) collective-permute-start(bf16[1536,256]{1,0:T(8,128)(2,1)S(1)} %pad_maximum_fusion.2), channel_id=1, source_target_pairs={{0,16},{8,24},{16,0},{24,8},{32,48},{40,56},{48,32},{56,40},{64,80... | collective-permute-start | bytes 2359304 | tf_op jit(solution)/shard_map/ppermute | solution.py:11
  422.9 16.6 %collective-permute-start.9 = (bf16[1536,256]{0,1:T(8,128)(2,1)S(1)}, bf16[1536,256]{0,1:T(8,128)(2,1)S(1)}, u32[]{:S(2)}, u32[]{:S(2)}) collective-permute-start(bf16[1536,256]{0,1:T(8,128)(2,1)S(1)} %convert_element_type.93), channel_id=1, source_target_pairs={{0,8},{8,0},{16,24},{24,16},{32,40},{40,32},{48,56},{56,48},{64,72... | collective-permute-start | bytes 2359304 | tf_op jit(solution)/shard_map/ppermute | solution.py:11
  439.7 19.1 %collective-permute-start.10 = (bf16[1536,256]{0,1:T(8,128)(2,1)S(1)}, bf16[1536,256]{0,1:T(8,128)(2,1)S(1)}, u32[]{:S(2)}, u32[]{:S(2)}) collective-permute-start(bf16[1536,256]{0,1:T(8,128)(2,1)S(1)} %fusion.15), channel_id=1, source_target_pairs={{0,16},{8,24},{16,0},{24,8},{32,48},{40,56},{48,32},{56,40},{64,80... | collective-permute-start | bytes 2359304 | tf_op jit(solution)/shard_map/ppermute | solution.py:11
  443.9 32.5 %collective-permute-start.8 = (bf16[3072,256]{1,0:T(8,128)(2,1)}, bf16[3072,256]{1,0:T(8,128)(2,1)}, u32[]{:S(2)}, u32[]{:S(2)}) collective-permute-start(bf16[3072,256]{1,0:T(8,128)(2,1)} %pad_maximum_fusion.1), channel_id=1, source_target_pairs={{0,32},{8,40},{16,48},{24,56},{32,0},{40,8},{48,16},{56,24},{64,96... | collective-permute-start | bytes 4718600 | tf_op jit(solution)/shard_map/ppermute | solution.py:11
  460.3 49.8 %collective-permute-start.11 = (f32[1536,256]{0,1:T(8,128)}, f32[1536,256]{0,1:T(8,128)}, u32[]{:S(2)}, u32[]{:S(2)}) collective-permute-start(f32[1536,256]{0,1:T(8,128)} %convert_add_fusion.2), channel_id=1, source_target_pairs={{0,32},{8,40},{16,48},{24,56},{32,0},{40,8},{48,16},{56,24},{64,96... | collective-permute-start | bytes 4718600 | tf_op jit(solution)/shard_map/ppermute | solution.py:11
  593.9 16.6 %collective-permute-start.12 = (bf16[1536,256]{0,1:T(8,128)(2,1)S(1)}, bf16[1536,256]{0,1:T(8,128)(2,1)S(1)}, u32[]{:S(2)}, u32[]{:S(2)}) collective-permute-start(bf16[1536,256]{0,1:T(8,128)(2,1)S(1)} %convert_element_type.100), channel_id=1, source_target_pairs={{0,8},{8,0},{16,24},{24,16},{32,40},{40,32},{48,56},{56,48},{64,72... | collective-permute-start | bytes 2359304 | tf_op jit(solution)/shard_map/ppermute | solution.py:11
  610.7 19.1 %collective-permute-start.13 = (bf16[1536,256]{0,1:T(8,128)(2,1)S(1)}, bf16[1536,256]{0,1:T(8,128)(2,1)S(1)}, u32[]{:S(2)}, u32[]{:S(2)}) collective-permute-start(bf16[1536,256]{0,1:T(8,128)(2,1)S(1)} %fusion.16), channel_id=1, source_target_pairs={{0,16},{8,24},{16,0},{24,8},{32,48},{40,56},{48,32},{56,40},{64,80... | collective-permute-start | bytes 2359304 | tf_op jit(solution)/shard_map/ppermute | solution.py:11
  631.3 15.8 %collective-permute-start.14 = (bf16[1536,256]{0,1:T(8,128)(2,1)S(1)}, bf16[1536,256]{0,1:T(8,128)(2,1)}, u32[]{:S(2)}, u32[]{:S(2)}) collective-permute-start(bf16[1536,256]{0,1:T(8,128)(2,1)S(1)} %get-tuple-element.15), channel_id=1, source_target_pairs={{0,32},{8,40},{16,48},{24,56},{32,0},{40,8},{48,16},{56,24},{64,96... | collective-permute-start | bytes 2359304 | tf_op jit(solution)/shard_map/ppermute | solution.py:11
  (30 other events, 206.6 us)
Sparse Core Ops, SparseCore 0:
  9.7 27.8 all-gather.4
  39.3 27.8 all-gather.2
  77.3 61.6 all-reduce.4
  188.1 66.8 all-reduce.6
  356.6 64.7 all-reduce.8
  523.7 68.5 all-reduce.10
where the time goes:
time: 668 us; the launch traced here: 656 us
  waiting for transfers between devices  466 us (70%)
  local copies, waits for them, and re-layouts  46.7 us (7%)
  matrix products  36.7 us (5%)
  blocking collectives  35.7 us (5%)
  other arithmetic  32.2 us (5%)
  starting transfers between devices  23.6 us (4%)
  between operations  14.9 us (2%)
    psum x4, waiting for transfers between devices, reduce_whole(): summed = lax.psum(partial_value, 'rows')  259 us
    ppermute x15, waiting for transfers between devices, partner_2(): lax.ppermute(value, axis, [(i, i ^ 1 << apart) for i in range(lax.axis_si...  148 us
    all_gather x2, waiting for transfers between devices, stack_group(): gathered = lax.all_gather(local_rows, 'rows', axis=0, tiled=True)  57.2 us
    all_gather x2, blocking collectives, stack_group(): gathered = lax.all_gather(local_rows, 'rows', axis=0, tiled=True)  35.7 us
    dot_general x6, local copies, waits for them, and re-layouts, place_rows(): jnp.einsum('us,ubn->sbn', selector, blocks, precision=lax.Precision.HIGHEST)  30.7 us
    ppermute x15, starting transfers between devices, partner_2(): lax.ppermute(value, axis, [(i, i ^ 1 << apart) for i in range(lax.axis_si...  23.4 us
    dot_general x6, matrix products, place_rows(): jnp.einsum('us,ubn->sbn', selector, blocks, precision=lax.Precision.HIGHEST)  19.4 us
    select_n x6, other arithmetic, stack_group(): lower_part = jnp.where(is_upper, partner, gathered)  13.5 us
  transfers between devices with their start and end apart: 21, of which 18 were waited for; matrix products, arithmetic and copies ran while one was open for 14% of the time, Pallas kernels for 0%

commit v1 on v0

v1 whole, which is shorter than its diff:
```python
import jax
import jax.numpy as jnp
from jax import lax
from jax.experimental import pallas as pl
from jax.experimental.pallas import tpu as pltpu
from jax.sharding import PartitionSpec as P

S = 6144
N = 256
UR = 1536
BLK = 128
UB = 12
SB = S // BLK
HALF = 128
ROWS = (768, 384, 192, 96)
MESH = pl.DeviceIdType.MESH
F32 = jnp.float32
BF16 = jnp.bfloat16

DIM = {"y1": (0, 0, 1), "y3": (0, 0, 3), "z1": (0, 1, 0), "z3": (0, 3, 0), "x1": (1, 0, 0)}

REDUCE = (
    (("y1", "y3"), ("y3", "y1")),
    (("y1", "y3", "z1"), ("z1", "y1", "y3")),
    (("y1", "y3", "z1", "z3"), ("z1", "z3", "y1", "y3")),
    (("y1", "y3", "z1", "z3", "x1"), ("z1", "z3", "y1", "y3", "x1")),
)
SIBLING = ("z1", "z3", "x1")

GATHER = {
    1: (("y1", "y3", "z1"), ("z1", "y1", "y3")),
    2: (("y1", "y3", "z1", "z3"), ("z1", "z3", "y1", "y3")),
    3: (("y1", "y3", "z1", "z3", "x1"), ("x1", "z1", "z3", "y1", "y3")),
}
NX = {1: 1, 2: 1, 3: 2}
NZ = {1: 2, 2: 4, 3: 4}
NCH = 2
PCH = 4


def flip(value, mask):
    if mask == 0:
        return value
    if mask == 1:
        return value + 1 - 2 * (value % 2)
    if mask == 2:
        return (value + 2) % 4
    return 3 - value


def bit_of(name, x, z, y):
    if name == "y1":
        return ((y + 1) // 2) % 2
    if name == "y3":
        return y // 2
    if name == "z1":
        return ((z + 1) // 2) % 2
    if name == "z3":
        return z // 2
    return x % 2


def xor(a, b):
    return tuple(i ^ j for i, j in zip(a, b))


def held_before(order, step):
    held = [(0, 0, 0)]
    for name in order[:step]:
        held = held + [xor(h, DIM[name]) for h in held]
    return held


def mask_id(mask):
    return mask[0] * 16 + mask[1] * 4 + mask[2]


class Counter:
    def __init__(self):
        self.used = 0

    def take(self, count=1):
        first = self.used
        self.used += count
        return first


N_SEM = 560
N_LOCAL = 32


def kernel(*refs):
    loads = refs[0:4]
    inverse = refs[4:8]
    panel = refs[8:12]
    tables = (None,) + tuple(refs[12:15])
    outs = refs[15:19]
    out_anc = refs[19]
    scratch = list(refs[20:])

    def pop(count):
        taken = scratch[:count]
        del scratch[:count]
        return taken

    inv = pop(4)
    pan = pop(4)
    first = pop(1)[0]
    lbuf = [None] + pop(3)
    ubuf = pop(3)
    solved = pop(4)
    acc0 = pop(1)[0]
    acc_l = [None] + pop(3)
    cols = [None] + pop(3)
    part, acc = pop(2)
    dsend = pop(4)
    drecv = pop(4)
    stage = [pop(len(REDUCE[k][0])) for k in range(4)]
    arrived = [pop(len(REDUCE[k][0])) for k in range(4)]
    fin_send, fin_recv, anc = pop(3)
    ssem, rsem, lsem = pop(3)

    leaf = lax.axis_index("leaf")
    rows = lax.axis_index("rows")
    x, z, y, c = leaf // 4, leaf % 4, rows // 2, rows % 2
    counter = Counter()
    local = Counter()
    sent = []

    def dev(mask, other_core=False):
        core = 1 - c if other_core else c
        return (flip(x, mask[0]) * 4 + flip(z, mask[1]), flip(y, mask[2]) * 2 + core)

    def by_core(zero, one):
        return tuple(a + c * (b - a) for a, b in zip(zero, one))

    sib = dev((0, 0, 0), True)

    def send(src, dst, si, ri, device):
        pltpu.make_async_remote_copy(
            src_ref=src, dst_ref=dst, send_sem=ssem.at[si], recv_sem=rsem.at[ri],
            device_id=device, device_id_type=MESH,
        ).start()

    def wait_recv(dst, ri):
        pltpu.make_async_remote_copy(
            src_ref=dst, dst_ref=dst, send_sem=ssem.at[0], recv_sem=rsem.at[ri],
            device_id=sib, device_id_type=MESH,
        ).wait_recv()

    def wait_send(src, si):
        pltpu.make_async_remote_copy(
            src_ref=src, dst_ref=src, send_sem=ssem.at[si], recv_sem=rsem.at[0],
            device_id=sib, device_id_type=MESH,
        ).wait_send()

    def fetch(src, dst):
        copy = pltpu.make_async_copy(src, dst, lsem.at[local.take()])
        copy.start()
        return copy

    def fetch_blocks(k):
        sem = lsem.at[local.take()]
        for t in range(SB):
            pltpu.make_async_copy(
                inverse[k].at[:, t * BLK:(t + 1) * BLK], inv[k].at[t], sem
            ).start()
        return pltpu.make_async_copy(inv[k], inv[k], sem)

    barrier = pltpu.get_barrier_semaphore()
    partners = [sib] + [dev(DIM[name]) for name in ("y1", "y3", "z1", "z3", "x1")]
    for partner in partners:
        pl.semaphore_signal(barrier, inc=1, device_id=partner, device_id_type=MESH)
    pl.semaphore_wait(barrier, len(partners))

    ch_rows = ROWS[0] // NCH
    g_recv = {m: counter.take(NCH) for m in (1, 2, 3)}
    g_fwd = {m: counter.take(NCH) for m in (0, 1, 2, 3)}
    g_send = {m: counter.take(NCH) for m in (1, 2, 3)}
    g_fsend = {m: counter.take(NCH) for m in (0, 1, 2, 3)}

    def first_at(mask, ch, core):
        return first.at[flip(y, mask), core, pl.ds(ch * ch_rows, ch_rows)]

    for ch in range(NCH):
        src = loads[0].at[pl.ds(ch * ch_rows, ch_rows)]
        for m in (1, 3):
            send(src, first_at(0, ch, c), g_send[m] + ch, g_recv[m] + ch, dev((0, 0, m)))
            sent.append((src, g_send[m] + ch))
    for ch in range(NCH):
        src = loads[0].at[pl.ds(ch * ch_rows, ch_rows)]
        send(src, first_at(0, ch, c), g_fsend[0] + ch, g_fwd[0] + ch, sib)
        sent.append((src, g_fsend[0] + ch))
    own_first = fetch(loads[0], first.at[y, c])
    inv_copy = [fetch(inverse[0], inv[0])]
    pan_copy = [fetch(panel[0], pan[0])]

    l_recv = {k: counter.take(32) for k in (1, 2, 3)}
    l_fwd = {k: counter.take(32) for k in (1, 2, 3)}
    l_send = {k: counter.take(32) for k in (1, 2, 3)}
    l_fsend = {k: counter.take(32) for k in (1, 2, 3)}

    def l_at(k, mask, core):
        xi = flip(x, mask[0]) % 2 if k == 3 else 0
        zi = flip(z, mask[1]) % NZ[k]
        return lbuf[k].at[xi, zi, flip(y, mask[2]), core]

    def l_source(k, mask):
        return loads[k] if mask == (0, 0, 0) else l_at(k, mask, c)

    def l_step(k, step):
        for core in (0, 1):
            @pl.when(c == core)
            def _(core=core):
                order = GATHER[k][core]
                if step > 0:
                    l_collect(k, order, step - 1)
                dim = DIM[order[step]]
                for held in held_before(order, step):
                    there = xor(held, dim)
                    send(l_source(k, held), l_at(k, held, c), l_send[k] + mask_id(there),
                         l_recv[k] + mask_id(there), dev(dim))

    def l_collect(k, order, step):
        dim = DIM[order[step]]
        for held in held_before(order, step):
            here = xor(held, dim)
            wait_recv(l_at(k, here, c), l_recv[k] + mask_id(here))
            send(l_at(k, here, c), l_at(k, here, c), l_fsend[k] + mask_id(here),
                 l_fwd[k] + mask_id(here), sib)

    def all_masks(k):
        zs = (0, 1) if k == 1 else (0, 1, 2, 3)
        xs = (0, 1) if k == 3 else (0,)
        return [(xm, zm, ym) for xm in xs for zm in zs for ym in range(4)]

    l_own = {}

    def l_begin(k):
        send(loads[k], l_at(k, (0, 0, 0), c), l_fsend[k], l_fwd[k], sib)
        l_own[k] = fetch(loads[k], l_at(k, (0, 0, 0), c))
        for mask in all_masks(k):
            sent.append((loads[k], l_fsend[k] + mask_id(mask)))
            if mask != (0, 0, 0):
                sent.append((loads[k], l_send[k] + mask_id(mask)))

    def l_finish(k):
        for core in (0, 1):
            @pl.when(c == core)
            def _(core=core):
                order = GATHER[k][core]
                l_collect(k, order, len(order) - 1)
        l_own[k].wait()
        for mask in all_masks(k):
            wait_recv(l_at(k, mask, 1 - c), l_fwd[k] + mask_id(mask))

    def l_product(k):
        inv_copy[k].wait()
        whole = jnp.concatenate([inv[k][t] for t in range(SB)], axis=1)
        acc_l[k][...] = jnp.dot(
            whole, lbuf[k][...].reshape(S, N), preferred_element_type=F32
        )

    def gather_columns(k):
        parent = leaf // (2 ** k)
        for j in range(2):
            for i in range(UB):
                t = tables[k][2 * parent + j, i]
                cols[k][j, :, i * BLK:(i + 1) * BLK] = inv[k][t]

    for k in (1, 2, 3):
        l_begin(k)
        l_step(k, 0)
    for k in (1, 2, 3):
        inv_copy.append(fetch_blocks(k))
        pan_copy.append(fetch(panel[k], pan[k]))

    def multiply(mask, same_core):
        yy = flip(y, mask)
        core = c if same_core else 1 - c
        block = 2 * yy + core
        col = pl.multiple_of(block * ROWS[0], ROWS[0])

        @pl.when(block <= rows)
        def _():
            acc0[...] += jnp.dot(
                inv[0][:, pl.ds(col, ROWS[0])], first[yy, core], preferred_element_type=F32
            )

    def g_take(mask):
        for ch in range(NCH):
            ref = first_at(mask, ch, c)
            wait_recv(ref, g_recv[mask] + ch)
            if mask in (1, 3):
                core, onward = (0, 3) if mask == 1 else (1, 1)

                @pl.when(c == core)
                def _():
                    send(ref, ref, g_send[2] + ch, g_recv[2] + ch, dev((0, 0, onward)))
            send(ref, ref, g_fsend[mask] + ch, g_fwd[mask] + ch, sib)
            sent.append((ref, g_fsend[mask] + ch))
            if mask == 2:
                sent.append((ref, g_send[2] + ch))

    def g_other(mask):
        for ch in range(NCH):
            wait_recv(first_at(mask, ch, 1 - c), g_fwd[mask] + ch)

    acc0[...] = jnp.zeros_like(acc0)
    own_first.wait()
    inv_copy[0].wait()
    multiply(0, True)
    g_other(0)
    multiply(0, False)
    g_take(1)
    g_take(3)
    l_step(1, 1)
    multiply(1, True)
    multiply(3, True)
    g_other(1)
    multiply(1, False)
    g_other(3)
    multiply(3, False)
    g_take(2)
    multiply(2, True)
    g_other(2)
    multiply(2, False)
    solved[0][...] = acc0[...].astype(BF16)
    out_copies = [fetch(solved[0], outs[0])]

    def panel_product(k):
        pan_copy[k].wait()
        base_s, base_r = counter.take(PCH), counter.take(PCH)
        size = UR // PCH
        for i in range(PCH):
            at = pl.ds(i * size, size)
            value = jnp.dot(pan[k][at, :], solved[k][...], preferred_element_type=F32)
            low, high = value[:, :HALF], value[:, HALF:]
            dsend[k][at, :] = jnp.where(c == 0, high, low).astype(BF16)
            send(dsend[k].at[at], drecv[k].at[at], base_s + i, base_r + i, sib)
            sent.append((dsend[k].at[at], base_s + i))
            part[at, :] = jnp.where(c == 0, low, high)
        return base_r

    def add_cores(k, base_r):
        size = UR // PCH
        for i in range(PCH):
            at = pl.ds(i * size, size)
            wait_recv(drecv[k].at[at], base_r + i)
            if k < 3:
                acc[at, :] = part[at, :] + drecv[k][at, :].astype(F32)
        if k == 3:
            unit = UR // 32
            for xi in range(2):
                for zi in range(4):
                    for yi in range(4):
                        pos = []
                        for order in REDUCE[3]:
                            value = 0
                            for name in order:
                                value = 2 * value + bit_of(name, xi, zi, yi)
                            pos.append(value)
                        to = (pos[0] + c * (pos[1] - pos[0])) * unit
                        at = pl.ds((xi * 16 + zi * 4 + yi) * unit, unit)
                        acc[pl.ds(pl.multiple_of(to, unit), unit), :] = (
                            part[at, :] + drecv[3][at, :].astype(F32)
                        )

    def bit_at(names):
        zero, one = (bit_of(name, x, z, y) for name in names)
        return zero + c * (one - zero)

    def dev_at(names):
        return by_core(dev(DIM[names[0]]), dev(DIM[names[1]]))

    def reduce_level(k):
        offset, size = 0, UR
        for i, names in enumerate(zip(*REDUCE[k])):
            size //= 2
            bit = bit_at(names)
            give = pl.multiple_of(offset + (1 - bit) * size, size)
            keep = pl.multiple_of(offset + bit * size, size)
            stage[k][i][...] = acc[pl.ds(give, size), :].astype(BF16)
            si, ri = counter.take(), counter.take()
            send(stage[k][i], arrived[k][i], si, ri, dev_at(names))
            sent.append((stage[k][i], si))
            wait_recv(arrived[k][i], ri)
            acc[pl.ds(keep, size), :] += arrived[k][i][...].astype(F32)
            offset = keep
        return offset, size

    def spread_level(k, offset, size, between):
        own = (leaf // (2 ** k)) % 2
        u = ubuf[k]
        forwards = []

        def forward(ref_of):
            si, ri = counter.take(), counter.take()
            send(ref_of, ref_of, si, ri, sib)
            sent.append((ref_of, si))
            forwards.append((ref_of, ri))

        at = pl.ds(pl.multiple_of(offset, size), size)
        u[own, c, at, :] = acc[at, :].astype(BF16)
        si, ri = counter.take(), counter.take()
        send(u.at[own, c, at], u.at[own, c, at], si, ri, dev(DIM[SIBLING[k]]))
        sent.append((u.at[own, c, at], si))
        wait_recv(u.at[1 - own, c, at], ri)
        forward(u.at[:, c, at])
        pairs = list(zip(*REDUCE[k]))
        for i in reversed(range(len(pairs))):
            bit = bit_at(pairs[i])
            at = pl.ds(pl.multiple_of(offset, size), size)
            other = pl.ds(pl.multiple_of(offset + (1 - 2 * bit) * size, size), size)
            si, ri = counter.take(), counter.take()
            send(u.at[:, c, at], u.at[:, c, at], si, ri, dev_at(pairs[i]))
            sent.append((u.at[:, c, at], si))
            if i == 0:
                between()
            wait_recv(u.at[:, c, other], ri)
            forward(u.at[:, c, other])
            offset = offset - bit * size
            size *= 2
        for ref_of, ri in forwards:
            wait_recv(ref_of, ri)

    def solve(k):
        total = acc_l[k][...]
        for j in range(2):
            rhs = jnp.concatenate([ubuf[k - 1][j, 0], ubuf[k - 1][j, 1]], axis=1)
            total = total - jnp.dot(cols[k][j], rhs, preferred_element_type=F32)
        solved[k][...] = total.astype(BF16)
        out_copies.append(fetch(solved[k], outs[k]))

    def before_last(k):
        def run():
            l_finish(k)
            l_product(k)
            gather_columns(k)
        return run

    for k in range(4):
        base = panel_product(k)
        if k == 0:
            l_step(1, 2)
            l_step(2, 1)
            l_step(3, 1)
        if k == 1:
            l_step(2, 3)
            l_step(3, 3)
        if k == 2:
            l_step(3, 4)
        add_cores(k, base)
        offset, size = reduce_level(k)
        if k == 0:
            l_step(2, 2)
            l_step(3, 2)
        if k < 3:
            spread_level(k, offset, size, before_last(k + 1))
            solve(k + 1)

    own_rows = acc[pl.ds(pl.multiple_of(offset + c * 24, 8), 24), :]
    fin_send[...] = acc[pl.ds(pl.multiple_of(offset + (1 - c) * 24, 8), 24), :]
    si, ri = counter.take(), counter.take()
    send(fin_send, fin_recv, si, ri, sib)
    sent.append((fin_send, si))
    wait_recv(fin_recv, ri)
    other_rows = fin_recv[...]
    anc[:, :HALF] = jnp.where(c == 0, own_rows, other_rows)
    anc[:, HALF:] = jnp.where(c == 0, other_rows, own_rows)
    out_copies.append(fetch(anc, out_anc))
    for src, si in sent:
        wait_send(src, si)
    for copy in out_copies:
        copy.wait()
    assert counter.used <= N_SEM and local.used <= N_LOCAL, (counter.used, local.used)


def per_device(*args):
    vmem = pltpu.VMEM
    scratch = [vmem((ROWS[0], S), BF16)] + [vmem((SB, r, BLK), BF16) for r in ROWS[1:]]
    scratch += [vmem((UR, r), BF16) for r in ROWS]
    scratch += [vmem((4, 2, ROWS[0], N), BF16)]
    scratch += [vmem((NX[k], NZ[k], 4, 2, ROWS[k], N), BF16) for k in (1, 2, 3)]
    scratch += [vmem((2, 2, UR, HALF), BF16) for _ in range(3)]
    scratch += [vmem((r, N), BF16) for r in ROWS]
    scratch += [vmem((ROWS[0], N), F32)]
    scratch += [vmem((ROWS[k], N), F32) for k in (1, 2, 3)]
    scratch += [vmem((2, ROWS[k], UR), BF16) for k in (1, 2, 3)]
    scratch += [vmem((UR, HALF), F32)] * 2
    scratch += [vmem((UR, HALF), BF16)] * 8
    for _ in range(2):
        for k in range(4):
            scratch += [vmem((UR >> (i + 1), HALF), BF16) for i in range(len(REDUCE[k][0]))]
    scratch += [vmem((24, HALF), F32), vmem((24, HALF), F32), vmem((24, N), F32)]
    scratch += [
        pltpu.SemaphoreType.DMA((N_SEM,)),
        pltpu.SemaphoreType.DMA((N_SEM,)),
        pltpu.SemaphoreType.DMA((N_LOCAL,)),
    ]
    anywhere = pl.BlockSpec(memory_space=pl.ANY)
    return pl.pallas_call(
        kernel,
        out_shape=tuple(jax.ShapeDtypeStruct((r, N), BF16) for r in ROWS)
        + (jax.ShapeDtypeStruct((24, N), F32),),
        in_specs=[anywhere] * 12 + [pl.BlockSpec(memory_space=pltpu.SMEM)] * 3,
        out_specs=(anywhere,) * 5,
        scratch_shapes=scratch,
        compiler_params=pltpu.CompilerParams(
            collective_id=0, has_side_effects=True, vmem_limit_bytes=63 * 1024 * 1024
        ),
    )(*args)


def solution(mesh):
    split = P(("leaf", "rows"), None)
    in_specs = (split,) * 8 + (P(None, ("leaf", "rows")),) * 4 + (P(),) * 3
    return jax.shard_map(
        per_device, mesh=mesh, in_specs=in_specs, out_specs=(split,) * 5, check_vma=False
    )
```

time: 668 us -> 193 us (0.29); the launches traced: 656 us -> 193 us
  waiting for transfers between devices: 466 us -> 0 us
  Pallas kernels: 0 us -> 180 us
  matrix products: 36.7 us -> 0 us
  blocking collectives: 35.7 us -> 0 us
  local copies, waits for them, and re-layouts: 46.7 us -> 11.8 us
  other arithmetic: 32.2 us -> 0 us
  starting transfers between devices: 23.6 us -> 0 us
  between operations: 14.9 us -> 0.64 us
    psum x4 -> x0, waiting for transfers between devices: 259 us -> none  [reduce_whole(): summed = lax.psum(partial_value, 'rows')]
    pallas_call x0 -> x1, Pallas kernels: none -> 180 us  [per_device(): pl.pallas_call(kernel, out_shape=tuple((jax.ShapeDtypeStruct((r, N), BF16...]
    ppermute x15 -> x0, waiting for transfers between devices: 148 us -> none  [partner_2(): lax.ppermute(value, axis, [(i, i ^ 1 << apart) for i in range(lax.axis_si...]
    all_gather x2 -> x0, waiting for transfers between devices: 57.2 us -> none  [stack_group(): gathered = lax.all_gather(local_rows, 'rows', axis=0, tiled=True)]
    dot_general x14 -> x0, matrix products: 36.7 us -> none  [the longest x6 19.4 us: place_rows(): jnp.einsum('us,ubn->sbn', selector, blocks, precision=lax.Precision.HIGHEST)]
    all_gather x2 -> x0, blocking collectives: 35.7 us -> none  [stack_group(): gathered = lax.all_gather(local_rows, 'rows', axis=0, tiled=True)]
    dot_general x6 -> x0, local copies, waits for them, and re-layouts: 30.7 us -> none  [place_rows(): jnp.einsum('us,ubn->sbn', selector, blocks, precision=lax.Precision.HIGHEST)]
    ppermute x15 -> x0, starting transfers between devices: 23.4 us -> none  [partner_2(): lax.ppermute(value, axis, [(i, i ^ 1 << apart) for i in range(lax.axis_si...]
  transfers between devices with their start and end apart: 21 -> 0, of which waited for: 18 -> 0; matrix products, arithmetic and copies ran while one was open for 14% -> 0% of each run, Pallas kernels for 0% -> 0%
where the time goes in v1:
time: 193 us
  Pallas kernels  180 us (93%)
  local copies, waits for them, and re-layouts  11.8 us (6%)
    pallas_call x1, Pallas kernels, per_device(): pl.pallas_call(kernel, out_shape=tuple((jax.ShapeDtypeStruct((r, N), BF16...  180 us
    unnamed x7, local copies, waits for them, and re-layouts  11.8 us

profile of v1, /device:TPU:1, one launch (start us, length us, event | category | flops | bytes accessed | tf_op | source)
XLA Modules:
  0.0 192.9 jit_solution(582965754982710100)
XLA Ops:
  0.6 1.9 copy.21.refs_11_
  2.5 2.2 %copy.20.refs_10_ = bf16[1536,192]{1,0:T(8,128)(2,1)} copy(bf16[1536,192]{0,1:T(8,128)(2,1)} %param.25) | data formatting | bytes 1179648 | tf_op args[10]
  4.7 180.4 %shard_map.182 = (bf16[768,256]{1,0:T(8,128)(2,1)}, bf16[384,256]{1,0:T(8,128)(2,1)}, bf16[192,256]{1,0:T(8,128)(2,1)}, bf16[96,256]{1,0:T(8,128)(2,1)}, f32[24,256]{1,0:T(8,128)}) custom-call(bf16[768,256]{1,0:T(8,128)(2,1)} %refs_0_.1, bf16[384,256]{1,0:T(8,128)(2,1)} %refs_1_.1, bf16[192,256]{1,0:T(8,128)(2,1)} %refs_2_.1, bf16[96,256]{1,0:T(8,128)(2,1)} %refs_3_.1, ...), custom_call_target="tpu_custom_call" | custom-call | tf_op jit(solution)/shard_map/pallas_call | solution.py:502
  185.2 1.8 copy.27
  186.9 1.6 copy.28
  188.6 1.5 copy.29
  190.1 1.4 copy.30
  191.5 1.3 copy.31

commit v2 on v1

v2 whole, which is shorter than its diff:
```python
import jax
import jax.numpy as jnp
from jax import lax
from jax.experimental import pallas as pl
from jax.experimental.pallas import tpu as pltpu
from jax.sharding import PartitionSpec as P

S = 6144
N = 256
UR = 1536
BLK = 128
UB = 12
SB = S // BLK
HALF = 128
ROWS = (768, 384, 192, 96)
MESH = pl.DeviceIdType.MESH
F32 = jnp.float32
BF16 = jnp.bfloat16

STAGE = {
    "y": ((0, 0, 2), (0, 0, 1), (0, 0, 3)),
    "z1": ((0, 1, 0),),
    "z3": ((0, 3, 0),),
    "x1": ((1, 0, 0),),
}

CHIPS = (4, 8, 16, 32)

GATHER = {1: ("y", "z1"), 2: ("y", "z1", "z3"), 3: ("y", "z3", "z1", "x1")}
Y_MASKS = STAGE["y"]
Z_MASKS = ((0, 2, 0), (0, 1, 0), (0, 3, 0))
SPREAD = (
    ((((0, 1, 0),), Y_MASKS), (Y_MASKS, ((0, 1, 0),))),
    ((Z_MASKS, Y_MASKS), (Y_MASKS, Z_MASKS)),
    (
        (tuple((1,) + m[1:] for m in Z_MASKS) + Z_MASKS + ((1, 0, 0),), Y_MASKS),
        (tuple((1,) + m[1:] for m in Y_MASKS) + Y_MASKS + ((1, 0, 0),), Z_MASKS),
    ),
)
NX = {1: 1, 2: 1, 3: 2}
NZ = {1: 2, 2: 4, 3: 4}
NCH = 3
PCH = 4


def flip(value, mask):
    if mask == 0:
        return value
    if mask == 1:
        return value + 1 - 2 * (value % 2)
    if mask == 2:
        return (value + 2) % 4
    return 3 - value


def xor(a, b):
    return tuple(i ^ j for i, j in zip(a, b))


def held_before(order, step):
    held = [(0, 0, 0)]
    for name in order[:step]:
        held = held + [xor(h, m) for m in STAGE[name] for h in held]
    return held


def mask_id(mask):
    return mask[0] * 16 + mask[1] * 4 + mask[2]


class Counter:
    def __init__(self):
        self.used = 0

    def take(self, count=1):
        first = self.used
        self.used += count
        return first


N_SEND = 48
N_RECV = 96
N_LOCAL = 32


def kernel(*refs):
    loads = refs[0:4]
    inverse = refs[4:8]
    panel = refs[8:12]
    tables = (None,) + tuple(refs[12:15])
    outs = refs[15:19]
    out_anc = refs[19]
    scratch = list(refs[20:])

    def pop(count):
        taken = scratch[:count]
        del scratch[:count]
        return taken

    inv = pop(4)
    pan = pop(4)
    first = pop(1)[0]
    lbuf = [None] + pop(3)
    ubuf = pop(3)
    solved = pop(4)
    acc0 = pop(1)[0]
    acc_l = [None] + pop(3)
    cols = [None] + pop(3)
    part = pop(1)[0]
    dsend = pop(4)
    drecv = pop(4)
    stage = pop(4)
    arrived = pop(4)
    pan_t = [None, None] + pop(2)
    fin_acc, fin_send, fin_recv, anc = pop(4)
    ssem, rsem, lsem = pop(3)

    leaf = lax.axis_index("leaf")
    rows = lax.axis_index("rows")
    x, z, y, c = leaf // 4, leaf % 4, rows // 2, rows % 2
    out_sem = Counter()
    in_sem = Counter()
    local = Counter()
    sent = []

    def dev(mask, other_core=False):
        core = 1 - c if other_core else c
        return (flip(x, mask[0]) * 4 + flip(z, mask[1]), flip(y, mask[2]) * 2 + core)

    sib = dev((0, 0, 0), True)

    def send(src, dst, si, ri, device):
        pltpu.make_async_remote_copy(
            src_ref=src, dst_ref=dst, send_sem=ssem.at[si], recv_sem=rsem.at[ri],
            device_id=device, device_id_type=MESH,
        ).start()

    def wait_recv(dst, ri):
        pltpu.make_async_remote_copy(
            src_ref=dst, dst_ref=dst, send_sem=ssem.at[0], recv_sem=rsem.at[ri],
            device_id=sib, device_id_type=MESH,
        ).wait_recv()

    def wait_send(src, si):
        pltpu.make_async_remote_copy(
            src_ref=src, dst_ref=src, send_sem=ssem.at[si], recv_sem=rsem.at[0],
            device_id=sib, device_id_type=MESH,
        ).wait_send()

    def fetch(src, dst):
        copy = pltpu.make_async_copy(src, dst, lsem.at[local.take()])
        copy.start()
        return copy

    def fetch_blocks(k):
        sem = lsem.at[local.take()]
        for t in range(SB):
            pltpu.make_async_copy(
                inverse[k].at[:, t * BLK:(t + 1) * BLK], inv[k].at[t], sem
            ).start()
        return pltpu.make_async_copy(inv[k], inv[k], sem)

    barrier = pltpu.get_barrier_semaphore()
    partners = [sib] + [
        dev((xm, zm, ym))
        for xm in range(2) for zm in range(4) for ym in range(4) if (xm, zm, ym) != (0, 0, 0)
    ]
    for partner in partners:
        pl.semaphore_signal(barrier, inc=1, device_id=partner, device_id_type=MESH)
    pl.semaphore_wait(barrier, len(partners))

    ch_rows = ROWS[0] // NCH
    g_recv = {m: in_sem.take(NCH) for m in (1, 2, 3)}
    g_fwd = {m: in_sem.take() for m in (0, 1, 2, 3)}
    g_send = {m: out_sem.take() for m in (1, 3)}
    g_relay = {m: out_sem.take() for m in (1, 3)}
    g_fsend = {m: out_sem.take() for m in (0, 1, 2, 3)}

    def first_at(mask, ch, core):
        return first.at[flip(y, mask), core, pl.ds(ch * ch_rows, ch_rows)]

    def below(mask):
        return flip(y, mask) < y

    def passes_on(core, block):
        return (c == core) & (block < flip(block, 2))

    l_recv = {k: in_sem.take(len(GATHER[k])) for k in (1, 2, 3)}
    l_fwd = {k: in_sem.take() for k in (1, 2, 3)}
    l_send = {k: out_sem.take(len(GATHER[k])) for k in (1, 2, 3)}
    l_fsend = {k: out_sem.take() for k in (1, 2, 3)}

    def l_bulk(k, step):
        ref = lbuf[k]
        count = len(STAGE[GATHER[k][step]]) * len(held_before(GATHER[k], step))
        if count == 3:
            return ref.at[0, 0, 0:3, 0]
        if count == 4:
            return ref.at[0, 0, :, 0]
        if count == 8:
            return ref.at[0, 0:2, :, 0]
        return ref.at[0, :, :, 0]

    def l_at(k, mask, core):
        xi = flip(x, mask[0]) % 2 if k == 3 else 0
        zi = flip(z, mask[1]) % NZ[k]
        return lbuf[k].at[xi, zi, flip(y, mask[2]), core]

    def l_source(k, mask):
        return loads[k] if mask == (0, 0, 0) else l_at(k, mask, c)

    def l_step(k, step):
        if step > 0:
            l_collect(k, step - 1)
        for mask in STAGE[GATHER[k][step]]:
            for held in held_before(GATHER[k], step):
                send(l_source(k, held), l_at(k, held, c), l_send[k] + step, l_recv[k] + step,
                     dev(mask))
        sent.append((l_bulk(k, step), l_send[k] + step, None))

    def l_collect(k, step):
        wait_recv(l_bulk(k, step), l_recv[k] + step)
        for mask in STAGE[GATHER[k][step]]:
            for held in held_before(GATHER[k], step):
                ref = l_at(k, xor(held, mask), c)
                send(ref, ref, l_fsend[k], l_fwd[k], sib)

    l_own = {}

    def l_begin(k):
        own = l_at(k, (0, 0, 0), c)
        send(loads[k], own, l_fsend[k], l_fwd[k], sib)
        l_own[k] = fetch(loads[k], own)
        sent.append((lbuf[k].at[:, :, :, 0], l_fsend[k], None))

    def l_finish(k):
        l_collect(k, len(GATHER[k]) - 1)
        l_own[k].wait()
        wait_recv(lbuf[k].at[:, :, :, 1 - c], l_fwd[k])

    def l_product(k):
        inv_copy[k].wait()
        whole = jnp.concatenate([inv[k][t] for t in range(SB)], axis=1)
        acc_l[k][...] = jnp.dot(
            whole, lbuf[k][...].reshape(S, N), preferred_element_type=F32
        )

    def gather_columns(k):
        parent = leaf // (2 ** k)
        for j in range(2):
            for i in range(UB):
                t = tables[k][2 * parent + j, i]
                at = j * UR + i * BLK
                cols[k][:, at:at + BLK] = inv[k][t]

    l_step(1, 0)
    for m, core in ((1, 0), (3, 1)):
        wanted = (y < flip(y, m)) | passes_on(core, y)

        @pl.when(wanted)
        def _():
            for ch in range(NCH):
                src = loads[0].at[pl.ds(ch * ch_rows, ch_rows)]
                send(src, first_at(0, ch, c), g_send[m], g_recv[m] + ch, dev((0, 0, m)))

        sent.append((loads[0], g_send[m], wanted))

    @pl.when(c == 0)
    def _():
        send(loads[0], first.at[y, c], g_fsend[0], g_fwd[0], sib)

    sent.append((loads[0], g_fsend[0], c == 0))
    own_first = fetch(loads[0], first.at[y, c])
    inv_copy = [fetch(inverse[0], inv[0])]
    pan_copy = [fetch(panel[0], pan[0])]
    for k in (1, 2, 3):
        l_begin(k)
        inv_copy.append(fetch_blocks(k))
        pan_copy.append(fetch(panel[k], pan[k] if k == 1 else pan_t[k]))

    def multiply(mask, same_core):
        yy = flip(y, mask)
        core = c if same_core else 1 - c
        col = pl.multiple_of((2 * yy + core) * ROWS[0], ROWS[0])
        acc0[...] += jnp.dot(
            inv[0][:, pl.ds(col, ROWS[0])], first[yy, core], preferred_element_type=F32
        )

    def g_take(mask):
        needed = below(mask)
        block = flip(y, mask)
        core, onward = (0, 3) if mask == 1 else (1, 1)
        relayed = passes_on(core, block) if mask != 2 else False

        for ch in range(NCH):
            ref = first_at(mask, ch, c)

            @pl.when(needed | relayed)
            def _():
                wait_recv(ref, g_recv[mask] + ch)

            if mask != 2:
                @pl.when(relayed)
                def _():
                    send(ref, ref, g_relay[mask], g_recv[2] + ch, dev((0, 0, onward)))

            @pl.when(needed)
            def _():
                send(ref, ref, g_fsend[mask], g_fwd[mask], sib)

        if mask != 2:
            sent.append((loads[0], g_relay[mask], relayed))
        sent.append((loads[0], g_fsend[mask], needed))

    def g_multiply(mask):
        @pl.when(below(mask))
        def _():
            multiply(mask, True)
            wait_recv(first.at[flip(y, mask), 1 - c], g_fwd[mask])
            multiply(mask, False)

    acc0[...] = jnp.zeros_like(acc0)
    own_first.wait()
    inv_copy[0].wait()
    multiply(0, True)

    @pl.when(c == 1)
    def _():
        wait_recv(first.at[y, 1 - c], g_fwd[0])
        multiply(0, False)

    l_step(1, 1)
    g_take(1)
    g_take(3)
    l_step(2, 0)
    l_step(3, 0)
    g_multiply(1)
    g_multiply(3)
    g_take(2)
    g_multiply(2)
    solved[0][...] = acc0[...].astype(BF16)
    out_copies = [fetch(solved[0], outs[0])]

    def place_of(k):
        return ((x % 2) * 16 + z * 4 + y) % CHIPS[k]

    def chip_of(k, place):
        whole = (x % 2) * 16 + z * 4 + y
        at = whole - whole % CHIPS[k] + place
        return ((x - x % 2 + at // 16) * 4 + (at // 4) % 4, (at % 4) * 2 + c)

    def update_level(k, between):
        chips, me = CHIPS[k], place_of(k)
        size = UR // chips
        if k < 2:
            pan_copy[k].wait()
        base_d, base_r = in_sem.take(PCH), in_sem.take()
        give_d, give_r = out_sem.take(), out_sem.take()
        rows_of = UR // PCH

        def finish(i):
            at = pl.ds(i * rows_of, rows_of)
            wait_recv(drecv[k].at[at], base_d + i)
            stage[k][at, :] = (part[at, :] + drecv[k][at, :].astype(F32)).astype(BF16)
            for q in range(i * chips // PCH, (i + 1) * chips // PCH):
                @pl.when(q != me)
                def _():
                    send(stage[k].at[pl.ds(q * size, size)], arrived[k].at[me],
                         give_r, base_r, chip_of(k, q))

        for i in range(PCH):
            at = pl.ds(i * rows_of, rows_of)
            value = jnp.dot(pan[k][at, :], solved[k][...], preferred_element_type=F32)
            low, high = value[:, :HALF], value[:, HALF:]
            dsend[k][at, :] = jnp.where(c == 0, high, low).astype(BF16)
            send(dsend[k].at[at], drecv[k].at[at], give_d, base_d + i, sib)
            part[at, :] = jnp.where(c == 0, low, high)
        for i in range(PCH):
            finish(i)
        between()
        mine = pl.ds(pl.multiple_of(me * size, size), size)
        total = part[mine, :] + drecv[k][mine, :].astype(F32)
        wait_recv(arrived[k].at[0:chips - 1], base_r)
        for i in range(1, chips):
            total = total + arrived[k][(me + i) % chips].astype(F32)
        sent.append((dsend[k], give_d, None))
        sent.append((arrived[k].at[0:chips - 1], give_r, None))
        return total

    def spread_level(k, total, between):
        chips = 2 * CHIPS[k]
        size = UR // CHIPS[k]
        u = ubuf[k]
        most = max(len(near) for near, _ in SPREAD[k])
        base_a, base_b, base_f = in_sem.take(most), in_sem.take(3), in_sem.take()
        give, give_f = out_sem.take(), out_sem.take()

        def piece(mask):
            at = (flip(x, mask[0]) % 2) * 16 + flip(z, mask[1]) * 4 + flip(y, mask[2])
            at = at % chips * size
            return u.at[c, pl.ds(pl.multiple_of(at, size), size)]

        def across(ref):
            send(ref, ref, give_f, base_f, sib)

        own = piece((0, 0, 0))
        own[...] = total.astype(BF16)
        for core, (near, far) in enumerate(SPREAD[k]):
            @pl.when(c == core)
            def _():
                for i, m in enumerate(near):
                    send(own, own, give, base_a + i, dev(m))
                for i, m in enumerate(far):
                    send(own, own, give, base_b + i, dev(m))
                across(own)
                for i in reversed(range(len(near))):
                    ref = piece(near[i])
                    wait_recv(ref, base_a + i)
                    for j, m in enumerate(far):
                        send(ref, ref, give, base_b + j, dev(m))
                    across(ref)

        between()
        for core, (near, far) in enumerate(SPREAD[k]):
            @pl.when(c == core)
            def _():
                for j in reversed(range(len(far))):
                    wait_recv(u.at[c, 0:(len(near) + 1) * size], base_b + j)
                    for m in ((0, 0, 0),) + near:
                        across(piece(xor(m, far[j])))

        sent.append((u.at[c, 0:(chips - 1) * size], give, None))
        sent.append((u.at[c], give_f, None))
        wait_recv(u.at[1 - c], base_f)
        rhs = jnp.concatenate([u[0], u[1]], axis=1)
        value = acc_l[k + 1][...] - jnp.dot(cols[k + 1][...], rhs, preferred_element_type=F32)
        solved[k + 1][...] = value.astype(BF16)
        out_copies.append(fetch(solved[k + 1], outs[k + 1]))

    def in_reduce(k):
        def run():
            if k == 0:
                for j in (2, 3):
                    pan_copy[j].wait()
                    pan[j][...] = pan_t[j][...].T
                l_step(3, 1)
                l_step(2, 1)
            if k == 1:
                l_step(3, 2)
        return run

    def in_spread(k):
        def run():
            if k == 0:
                l_step(2, 2)
            if k == 1:
                l_step(3, 3)
            l_finish(k + 1)
            l_product(k + 1)
            gather_columns(k + 1)
        return run

    for k in range(4):
        total = update_level(k, in_reduce(k))
        if k < 3:
            spread_level(k, total, in_spread(k))

    fin_acc[...] = total
    own_rows = fin_acc[pl.ds(pl.multiple_of(c * 24, 8), 24), :]
    fin_send[...] = fin_acc[pl.ds(pl.multiple_of((1 - c) * 24, 8), 24), :]
    si, ri = out_sem.take(), in_sem.take()
    send(fin_send, fin_recv, si, ri, sib)
    sent.append((fin_send, si, None))
    wait_recv(fin_recv, ri)
    other_rows = fin_recv[...]
    anc[:, :HALF] = jnp.where(c == 0, own_rows, other_rows)
    anc[:, HALF:] = jnp.where(c == 0, other_rows, own_rows)
    out_copies.append(fetch(anc, out_anc))
    for src, si, cond in sent:
        if cond is None:
            wait_send(src, si)
        else:
            pl.when(cond)(lambda src=src, si=si: wait_send(src, si))
    for copy in out_copies:
        copy.wait()
    used = (out_sem.used, in_sem.used, local.used)
    assert used <= (N_SEND, N_RECV, N_LOCAL) and max(used) <= N_RECV, used


def hand_over(*refs):
    given, taken, held, sem = refs[:5], refs[5:10], refs[10:15], refs[15]
    ins = [pltpu.make_async_copy(a, b, sem.at[i]) for i, (a, b) in enumerate(zip(given, held))]
    outs = [pltpu.make_async_copy(a, b, sem.at[5 + i]) for i, (a, b) in enumerate(zip(held, taken))]
    for copy in ins:
        copy.start()
    for first, second in zip(ins, outs):
        first.wait()
        second.start()
    for copy in outs:
        copy.wait()


def per_device(*args):
    vmem = pltpu.VMEM
    scratch = [vmem((ROWS[0], S), BF16)] + [vmem((SB, r, BLK), BF16) for r in ROWS[1:]]
    scratch += [vmem((UR, r), BF16) for r in ROWS]
    scratch += [vmem((4, 2, ROWS[0], N), BF16)]
    scratch += [vmem((NX[k], NZ[k], 4, 2, ROWS[k], N), BF16) for k in (1, 2, 3)]
    scratch += [vmem((2, 2 * UR, HALF), BF16) for _ in range(3)]
    scratch += [vmem((r, N), BF16) for r in ROWS]
    scratch += [vmem((ROWS[0], N), F32)]
    scratch += [vmem((ROWS[k], N), F32) for k in (1, 2, 3)]
    scratch += [vmem((ROWS[k], 2 * UR), BF16) for k in (1, 2, 3)]
    scratch += [vmem((UR, HALF), F32)]
    scratch += [vmem((UR, HALF), BF16)] * 12
    scratch += [vmem((n, UR // n, HALF), BF16) for n in CHIPS]
    scratch += [vmem((ROWS[k], UR), BF16) for k in (2, 3)]
    scratch += [vmem((48, HALF), F32), vmem((24, HALF), F32), vmem((24, HALF), F32), vmem((24, N), F32)]
    scratch += [
        pltpu.SemaphoreType.DMA((N_SEND,)),
        pltpu.SemaphoreType.DMA((N_RECV,)),
        pltpu.SemaphoreType.DMA((N_LOCAL,)),
    ]
    anywhere = pl.BlockSpec(memory_space=pl.ANY)
    shapes = tuple(jax.ShapeDtypeStruct((r, N), BF16) for r in ROWS)
    shapes += (jax.ShapeDtypeStruct((24, N), F32),)
    args = args[:10] + (args[10].T, args[11].T) + args[12:]
    results = pl.pallas_call(
        kernel,
        out_shape=shapes,
        in_specs=[anywhere] * 12 + [pl.BlockSpec(memory_space=pltpu.SMEM)] * 3,
        out_specs=(anywhere,) * 5,
        scratch_shapes=scratch,
        compiler_params=pltpu.CompilerParams(
            collective_id=0, has_side_effects=True, vmem_limit_bytes=63 * 1024 * 1024
        ),
    )(*args)
    return pl.pallas_call(
        hand_over,
        out_shape=shapes,
        in_specs=[anywhere] * 5,
        out_specs=(anywhere,) * 5,
        scratch_shapes=[vmem(a.shape, a.dtype) for a in shapes] + [pltpu.SemaphoreType.DMA((10,))],
    )(*results)


def solution(mesh):
    split = P(("leaf", "rows"), None)
    in_specs = (split,) * 8 + (P(None, ("leaf", "rows")),) * 4 + (P(),) * 3
    return jax.shard_map(
        per_device, mesh=mesh, in_specs=in_specs, out_specs=(split,) * 5, check_vma=False
    )
```

time: 193 us -> 129 us (0.67)
  Pallas kernels: 180 us -> 128 us
  local copies, waits for them, and re-layouts: 11.8 us -> 0 us
    pallas_call x1 -> x2, Pallas kernels: 180 us -> 128 us  [the longest x1 126 us: per_device(): pl.pallas_call(kernel, out_shape=shapes, in_specs=[anywhere] * 12 + [pl.B...]
    unnamed x7 -> x0, local copies, waits for them, and re-layouts: 11.8 us -> none
where the time goes in v2:
time: 129 us
  Pallas kernels  128 us (99%)
    pallas_call x1, Pallas kernels, per_device(): pl.pallas_call(kernel, out_shape=shapes, in_specs=[anywhere] * 12 + [pl.B...  126 us

profile of v2, /device:TPU:1, one launch (start us, length us, event | category | flops | bytes accessed | tf_op | source)
XLA Modules:
  0.0 128.7 jit_solution(18098083266564128800)
XLA Ops:
  0.6 125.9 %shard_map.182 = (bf16[768,256]{1,0:T(8,128)(2,1)}, bf16[384,256]{1,0:T(8,128)(2,1)}, bf16[192,256]{1,0:T(8,128)(2,1)}, bf16[96,256]{1,0:T(8,128)(2,1)}, f32[24,256]{1,0:T(8,128)}) custom-call(bf16[768,256]{1,0:T(8,128)(2,1)} %refs_0_.1, bf16[384,256]{1,0:T(8,128)(2,1)} %refs_1_.1, bf16[192,256]{1,0:T(8,128)(2,1)} %refs_2_.1, bf16[96,256]{1,0:T(8,128)(2,1)} %refs_3_.1, ...), custom_call_target="tpu_custom_call" | custom-call | tf_op jit(solution)/shard_map/pallas_call | solution.py:528
  126.6 1.9 %shard_map.183 = (bf16[768,256]{1,0:T(8,128)(2,1)}, bf16[384,256]{1,0:T(8,128)(2,1)}, bf16[192,256]{1,0:T(8,128)(2,1)}, bf16[96,256]{1,0:T(8,128)(2,1)}, f32[24,256]{1,0:T(8,128)}) custom-call(bf16[768,256]{1,0:T(8,128)(2,1)} %get-tuple-element.10.refs_0_, bf16[384,256]{1,0:T(8,128)(2,1)} %get-tuple-element.11.refs_1_, ...), custom_call_target="tpu_custom_call" | custom-call | tf_op jit(solution)/shard_map/pallas_call | solution.py:538

commit v3 on v2

--- a/solution.py
+++ b/solution.py
@@ -161,10 +161,10 @@
         return pltpu.make_async_copy(inv[k], inv[k], sem)
 
     barrier = pltpu.get_barrier_semaphore()
-    partners = [sib] + [
-        dev((xm, zm, ym))
-        for xm in range(2) for zm in range(4) for ym in range(4) if (xm, zm, ym) != (0, 0, 0)
-    ]
+    hops = (0, 1, 2, 1)
+    others = [(xm, zm, ym) for xm in range(2) for zm in range(4) for ym in range(4)][1:]
+    others.sort(key=lambda m: -(m[0] + hops[m[1]] + hops[m[2]]))
+    partners = [dev(m) for m in others] + [sib]
     for partner in partners:
         pl.semaphore_signal(barrier, inc=1, device_id=partner, device_id_type=MESH)
     pl.semaphore_wait(barrier, len(partners))
@@ -234,18 +234,17 @@
         sent.append((lbuf[k].at[:, :, :, 0], l_fsend[k], None))
 
     def l_finish(k):
-        l_collect(k, len(GATHER[k]) - 1)
         l_own[k].wait()
         wait_recv(lbuf[k].at[:, :, :, 1 - c], l_fwd[k])
 
     def l_product(k):
-        inv_copy[k].wait()
         whole = jnp.concatenate([inv[k][t] for t in range(SB)], axis=1)
         acc_l[k][...] = jnp.dot(
             whole, lbuf[k][...].reshape(S, N), preferred_element_type=F32
         )
 
     def gather_columns(k):
+        inv_copy[k].wait()
         parent = leaf // (2 ** k)
         for j in range(2):
             for i in range(UB):
@@ -286,31 +285,30 @@
             inv[0][:, pl.ds(col, ROWS[0])], first[yy, core], preferred_element_type=F32
         )
 
-    def g_take(mask):
+    def g_take(mask, ch):
         needed = below(mask)
         block = flip(y, mask)
         core, onward = (0, 3) if mask == 1 else (1, 1)
+        ref = first_at(mask, ch, c)
         relayed = passes_on(core, block) if mask != 2 else False
 
-        for ch in range(NCH):
-            ref = first_at(mask, ch, c)
-
-            @pl.when(needed | relayed)
+        @pl.when(needed | relayed)
+        def _():
+            wait_recv(ref, g_recv[mask] + ch)
+
+        if mask != 2:
+            @pl.when(relayed)
             def _():
-                wait_recv(ref, g_recv[mask] + ch)
-
+                send(ref, ref, g_relay[mask], g_recv[2] + ch, dev((0, 0, onward)))
+
+        @pl.when(needed)
+        def _():
+            send(ref, ref, g_fsend[mask], g_fwd[mask], sib)
+
+        if ch == 0:
             if mask != 2:
-                @pl.when(relayed)
-                def _():
-                    send(ref, ref, g_relay[mask], g_recv[2] + ch, dev((0, 0, onward)))
-
-            @pl.when(needed)
-            def _():
-                send(ref, ref, g_fsend[mask], g_fwd[mask], sib)
-
-        if mask != 2:
-            sent.append((loads[0], g_relay[mask], relayed))
-        sent.append((loads[0], g_fsend[mask], needed))
+                sent.append((loads[0], g_relay[mask], relayed))
+            sent.append((loads[0], g_fsend[mask], needed))
 
     def g_multiply(mask):
         @pl.when(below(mask))
@@ -330,13 +328,15 @@
         multiply(0, False)
 
     l_step(1, 1)
-    g_take(1)
-    g_take(3)
+    for ch in range(NCH):
+        g_take(1, ch)
+        g_take(3, ch)
     l_step(2, 0)
     l_step(3, 0)
     g_multiply(1)
     g_multiply(3)
-    g_take(2)
+    for ch in range(NCH):
+        g_take(2, ch)
     g_multiply(2)
     solved[0][...] = acc0[...].astype(BF16)
     out_copies = [fetch(solved[0], outs[0])]
@@ -443,23 +443,26 @@
                 for j in (2, 3):
                     pan_copy[j].wait()
                     pan[j][...] = pan_t[j][...].T
-                l_step(3, 1)
-                l_step(2, 1)
+                l_collect(1, 1)
             if k == 1:
-                l_step(3, 2)
+                l_step(3, 3)
+            if k < 3:
+                gather_columns(k + 1)
         return run
 
     def in_spread(k):
         def run():
             if k == 0:
                 l_step(2, 2)
-            if k == 1:
-                l_step(3, 3)
+                l_step(3, 2)
+            else:
+                l_collect(k + 1, len(GATHER[k + 1]) - 1)
             l_finish(k + 1)
             l_product(k + 1)
-            gather_columns(k + 1)
         return run
 
+    l_step(2, 1)
+    l_step(3, 1)
     for k in range(4):
         total = update_level(k, in_reduce(k))
         if k < 3:

time: 129 us -> 121 us (0.938)
  Pallas kernels: 128 us -> 120 us
    pallas_call x1, Pallas kernels: 126 us -> 118 us  [per_device(): pl.pallas_call(kernel, out_shape=shapes, in_specs=[anywhere] * 12 + [pl.B...]
where the time goes in v3:
time: 121 us
  Pallas kernels  120 us (99%)
    pallas_call x1, Pallas kernels, per_device(): pl.pallas_call(kernel, out_shape=shapes, in_specs=[anywhere] * 12 + [pl.B...  118 us

profile of v3, /device:TPU:1, one launch (start us, length us, event | category | flops | bytes accessed | tf_op | source)
XLA Modules:
  0.0 121.0 jit_solution(13273730347258510290)
XLA Ops:
  0.6 118.2 %shard_map.182 = (bf16[768,256]{1,0:T(8,128)(2,1)}, bf16[384,256]{1,0:T(8,128)(2,1)}, bf16[192,256]{1,0:T(8,128)(2,1)}, bf16[96,256]{1,0:T(8,128)(2,1)}, f32[24,256]{1,0:T(8,128)}) custom-call(bf16[768,256]{1,0:T(8,128)(2,1)} %refs_0_.1, bf16[384,256]{1,0:T(8,128)(2,1)} %refs_1_.1, bf16[192,256]{1,0:T(8,128)(2,1)} %refs_2_.1, bf16[96,256]{1,0:T(8,128)(2,1)} %refs_3_.1, ...), custom_call_target="tpu_custom_call" | custom-call | tf_op jit(solution)/shard_map/pallas_call | solution.py:531
  118.9 1.9 %shard_map.183 = (bf16[768,256]{1,0:T(8,128)(2,1)}, bf16[384,256]{1,0:T(8,128)(2,1)}, bf16[192,256]{1,0:T(8,128)(2,1)}, bf16[96,256]{1,0:T(8,128)(2,1)}, f32[24,256]{1,0:T(8,128)}) custom-call(bf16[768,256]{1,0:T(8,128)(2,1)} %get-tuple-element.10.refs_0_, bf16[384,256]{1,0:T(8,128)(2,1)} %get-tuple-element.11.refs_1_, ...), custom_call_target="tpu_custom_call" | custom-call | tf_op jit(solution)/shard_map/pallas_call | solution.py:541

commit v4 on v3

--- a/solution.py
+++ b/solution.py
@@ -41,6 +41,7 @@
 NZ = {1: 2, 2: 4, 3: 4}
 NCH = 3
 PCH = 4
+PARTS = (2, 2, 2, 1)
 
 
 def flip(value, mask):
@@ -79,7 +80,7 @@
 
 
 N_SEND = 48
-N_RECV = 96
+N_RECV = 112
 N_LOCAL = 32
 
 
@@ -167,6 +168,12 @@
     partners = [dev(m) for m in others] + [sib]
     for partner in partners:
         pl.semaphore_signal(barrier, inc=1, device_id=partner, device_id_type=MESH)
+    own_first = fetch(loads[0], first.at[y, c])
+    inv_copy = [fetch(inverse[0], inv[0])]
+    pan_copy = [fetch(panel[0], pan[0])]
+    for k in (1, 2, 3):
+        inv_copy.append(fetch_blocks(k))
+        pan_copy.append(fetch(panel[k], pan[k] if k == 1 else pan_t[k]))
     pl.semaphore_wait(barrier, len(partners))
 
     ch_rows = ROWS[0] // NCH
@@ -209,14 +216,22 @@
     def l_source(k, mask):
         return loads[k] if mask == (0, 0, 0) else l_at(k, mask, c)
 
-    def l_step(k, step):
-        if step > 0:
-            l_collect(k, step - 1)
-        for mask in STAGE[GATHER[k][step]]:
-            for held in held_before(GATHER[k], step):
-                send(l_source(k, held), l_at(k, held, c), l_send[k] + step, l_recv[k] + step,
-                     dev(mask))
-        sent.append((l_bulk(k, step), l_send[k] + step, None))
+    def l_step(k, step, cond=None):
+        def run():
+            if step > 0:
+                l_collect(k, step - 1)
+            for mask in STAGE[GATHER[k][step]]:
+                for held in held_before(GATHER[k], step):
+                    send(l_source(k, held), l_at(k, held, c), l_send[k] + step, l_recv[k] + step,
+                         dev(mask))
+
+        if cond is None:
+            run()
+        else:
+            pl.when(cond)(run)
+        if (k, step) not in l_done:
+            sent.append((l_bulk(k, step), l_send[k] + step, None))
+        l_done.add((k, step))
 
     def l_collect(k, step):
         wait_recv(l_bulk(k, step), l_recv[k] + step)
@@ -226,6 +241,7 @@
                 send(ref, ref, l_fsend[k], l_fwd[k], sib)
 
     l_own = {}
+    l_done = set()
 
     def l_begin(k):
         own = l_at(k, (0, 0, 0), c)
@@ -269,13 +285,8 @@
         send(loads[0], first.at[y, c], g_fsend[0], g_fwd[0], sib)
 
     sent.append((loads[0], g_fsend[0], c == 0))
-    own_first = fetch(loads[0], first.at[y, c])
-    inv_copy = [fetch(inverse[0], inv[0])]
-    pan_copy = [fetch(panel[0], pan[0])]
     for k in (1, 2, 3):
         l_begin(k)
-        inv_copy.append(fetch_blocks(k))
-        pan_copy.append(fetch(panel[k], pan[k] if k == 1 else pan_t[k]))
 
     def multiply(mask, same_core):
         yy = flip(y, mask)
@@ -354,7 +365,9 @@
         size = UR // chips
         if k < 2:
             pan_copy[k].wait()
-        base_d, base_r = in_sem.take(PCH), in_sem.take()
+        parts = PARTS[k]
+        part_size = size // parts
+        base_d, base_r = in_sem.take(PCH), in_sem.take(parts)
         give_d, give_r = out_sem.take(), out_sem.take()
         rows_of = UR // PCH
 
@@ -363,10 +376,13 @@
             wait_recv(drecv[k].at[at], base_d + i)
             stage[k][at, :] = (part[at, :] + drecv[k][at, :].astype(F32)).astype(BF16)
             for q in range(i * chips // PCH, (i + 1) * chips // PCH):
-                @pl.when(q != me)
-                def _():
-                    send(stage[k].at[pl.ds(q * size, size)], arrived[k].at[me],
-                         give_r, base_r, chip_of(k, q))
+                give_piece(q, 0)
+
+        def give_piece(q, h):
+            @pl.when(q != me)
+            def _():
+                send(stage[k].at[pl.ds(q * size + h * part_size, part_size)],
+                     arrived[k].at[h, me], give_r, base_r + h, chip_of(k, q))
 
         for i in range(PCH):
             at = pl.ds(i * rows_of, rows_of)
@@ -377,57 +393,74 @@
             part[at, :] = jnp.where(c == 0, low, high)
         for i in range(PCH):
             finish(i)
+        for h in range(1, parts):
+            for q in range(chips):
+                give_piece(q, h)
         between()
-        mine = pl.ds(pl.multiple_of(me * size, size), size)
-        total = part[mine, :] + drecv[k][mine, :].astype(F32)
-        wait_recv(arrived[k].at[0:chips - 1], base_r)
-        for i in range(1, chips):
-            total = total + arrived[k][(me + i) % chips].astype(F32)
         sent.append((dsend[k], give_d, None))
-        sent.append((arrived[k].at[0:chips - 1], give_r, None))
-        return total
-
-    def spread_level(k, total, between):
+        sent.append((arrived[k].at[:, 0:chips - 1], give_r, None))
+
+        def total_of(h):
+            at = pl.ds(pl.multiple_of(me * size + h * part_size, part_size), part_size)
+            total = part[at, :] + drecv[k][at, :].astype(F32)
+            wait_recv(arrived[k].at[h, 0:chips - 1], base_r + h)
+            for i in range(1, chips):
+                total = total + arrived[k][h, (me + i) % chips].astype(F32)
+            return total
+
+        return total_of
+
+    def spread_level(k, total_of, between):
         chips = 2 * CHIPS[k]
         size = UR // CHIPS[k]
         u = ubuf[k]
         most = max(len(near) for near, _ in SPREAD[k])
-        base_a, base_b, base_f = in_sem.take(most), in_sem.take(3), in_sem.take()
+        parts = PARTS[k]
+        part_size = size // parts
+        base_a, base_b = in_sem.take(most * parts), in_sem.take(3 * parts)
+        base_f = in_sem.take()
         give, give_f = out_sem.take(), out_sem.take()
 
-        def piece(mask):
+        def piece(mask, h):
             at = (flip(x, mask[0]) % 2) * 16 + flip(z, mask[1]) * 4 + flip(y, mask[2])
-            at = at % chips * size
-            return u.at[c, pl.ds(pl.multiple_of(at, size), size)]
+            at = at % chips * size + h * part_size
+            return u.at[c, pl.ds(pl.multiple_of(at, part_size), part_size)]
 
         def across(ref):
             send(ref, ref, give_f, base_f, sib)
 
-        own = piece((0, 0, 0))
-        own[...] = total.astype(BF16)
+        for h in range(parts):
+            own = piece((0, 0, 0), h)
+            own[...] = total_of(h).astype(BF16)
+            for core, (near, far) in enumerate(SPREAD[k]):
+                @pl.when(c == core)
+                def _():
+                    for i, m in enumerate(near):
+                        send(own, own, give, base_a + h * most + i, dev(m))
+                    for j, m in enumerate(far):
+                        send(own, own, give, base_b + h * 3 + j, dev(m))
+                    across(own)
+
         for core, (near, far) in enumerate(SPREAD[k]):
             @pl.when(c == core)
             def _():
-                for i, m in enumerate(near):
-                    send(own, own, give, base_a + i, dev(m))
-                for i, m in enumerate(far):
-                    send(own, own, give, base_b + i, dev(m))
-                across(own)
-                for i in reversed(range(len(near))):
-                    ref = piece(near[i])
-                    wait_recv(ref, base_a + i)
-                    for j, m in enumerate(far):
-                        send(ref, ref, give, base_b + j, dev(m))
-                    across(ref)
+                for h in range(parts):
+                    for i in reversed(range(len(near))):
+                        ref = piece(near[i], h)
+                        wait_recv(ref, base_a + h * most + i)
+                        for j, m in enumerate(far):
+                            send(ref, ref, give, base_b + h * 3 + j, dev(m))
+                        across(ref)
 
         between()
         for core, (near, far) in enumerate(SPREAD[k]):
             @pl.when(c == core)
             def _():
-                for j in reversed(range(len(far))):
-                    wait_recv(u.at[c, 0:(len(near) + 1) * size], base_b + j)
-                    for m in ((0, 0, 0),) + near:
-                        across(piece(xor(m, far[j])))
+                for h in range(parts):
+                    for j in reversed(range(len(far))):
+                        wait_recv(u.at[c, 0:(len(near) + 1) * part_size], base_b + h * 3 + j)
+                        for m in ((0, 0, 0),) + near:
+                            across(piece(xor(m, far[j]), h))
 
         sent.append((u.at[c, 0:(chips - 1) * size], give, None))
         sent.append((u.at[c], give_f, None))
@@ -443,6 +476,8 @@
                 for j in (2, 3):
                     pan_copy[j].wait()
                     pan[j][...] = pan_t[j][...].T
+                l_step(2, 1, y == 3)
+                l_step(3, 1, y == 3)
                 l_collect(1, 1)
             if k == 1:
                 l_step(3, 3)
@@ -461,14 +496,14 @@
             l_product(k + 1)
         return run
 
-    l_step(2, 1)
-    l_step(3, 1)
+    l_step(2, 1, y < 3)
+    l_step(3, 1, y < 3)
     for k in range(4):
-        total = update_level(k, in_reduce(k))
+        total_of = update_level(k, in_reduce(k))
         if k < 3:
-            spread_level(k, total, in_spread(k))
-
-    fin_acc[...] = total
+            spread_level(k, total_of, in_spread(k))
+
+    fin_acc[...] = total_of(0)
     own_rows = fin_acc[pl.ds(pl.multiple_of(c * 24, 8), 24), :]
     fin_send[...] = fin_acc[pl.ds(pl.multiple_of((1 - c) * 24, 8), 24), :]
     si, ri = out_sem.take(), in_sem.take()
@@ -516,7 +551,7 @@
     scratch += [vmem((ROWS[k], 2 * UR), BF16) for k in (1, 2, 3)]
     scratch += [vmem((UR, HALF), F32)]
     scratch += [vmem((UR, HALF), BF16)] * 12
-    scratch += [vmem((n, UR // n, HALF), BF16) for n in CHIPS]
+    scratch += [vmem((p, n, UR // n // p, HALF), BF16) for n, p in zip(CHIPS, PARTS)]
     scratch += [vmem((ROWS[k], UR), BF16) for k in (2, 3)]
     scratch += [vmem((48, HALF), F32), vmem((24, HALF), F32), vmem((24, HALF), F32), vmem((24, N), F32)]
     scratch += [

time: 121 us -> 116 us (0.959)
  Pallas kernels: 120 us -> 115 us
    pallas_call x1, Pallas kernels: 118 us -> 114 us  [per_device(): pl.pallas_call(kernel, out_shape=shapes, in_specs=[anywhere] * 12 + [pl.B...]
where the time goes in v4:
time: 116 us
  Pallas kernels  115 us (99%)
    pallas_call x1, Pallas kernels, per_device(): pl.pallas_call(kernel, out_shape=shapes, in_specs=[anywhere] * 12 + [pl.B...  114 us

profile of v4, /device:TPU:1, one launch (start us, length us, event | category | flops | bytes accessed | tf_op | source)
XLA Modules:
  0.0 116.3 jit_solution(9706935009419771446)
XLA Ops:
  0.6 113.6 %shard_map.182 = (bf16[768,256]{1,0:T(8,128)(2,1)}, bf16[384,256]{1,0:T(8,128)(2,1)}, bf16[192,256]{1,0:T(8,128)(2,1)}, bf16[96,256]{1,0:T(8,128)(2,1)}, f32[24,256]{1,0:T(8,128)}) custom-call(bf16[768,256]{1,0:T(8,128)(2,1)} %refs_0_.1, bf16[384,256]{1,0:T(8,128)(2,1)} %refs_1_.1, bf16[192,256]{1,0:T(8,128)(2,1)} %refs_2_.1, bf16[96,256]{1,0:T(8,128)(2,1)} %refs_3_.1, ...), custom_call_target="tpu_custom_call" | custom-call | tf_op jit(solution)/shard_map/pallas_call | solution.py:566
  114.2 1.9 %shard_map.183 = (bf16[768,256]{1,0:T(8,128)(2,1)}, bf16[384,256]{1,0:T(8,128)(2,1)}, bf16[192,256]{1,0:T(8,128)(2,1)}, bf16[96,256]{1,0:T(8,128)(2,1)}, f32[24,256]{1,0:T(8,128)}) custom-call(bf16[768,256]{1,0:T(8,128)(2,1)} %get-tuple-element.10.refs_0_, bf16[384,256]{1,0:T(8,128)(2,1)} %get-tuple-element.11.refs_1_, ...), custom_call_target="tpu_custom_call" | custom-call | tf_op jit(solution)/shard_map/pallas_call | solution.py:576

commit v5 on v4

--- a/solution.py
+++ b/solution.py
@@ -26,7 +26,11 @@
 
 CHIPS = (4, 8, 16, 32)
 
-GATHER = {1: ("y", "z1"), 2: ("y", "z1", "z3"), 3: ("y", "z3", "z1", "x1")}
+GATHER = {
+    1: (("y", "z1"), ("y", "z1")),
+    2: (("y", "z3", "z1"), ("y", "z1", "z3")),
+    3: (("y", "z1", "z3", "x1"), ("y", "z3", "z1", "x1")),
+}
 Y_MASKS = STAGE["y"]
 Z_MASKS = ((0, 2, 0), (0, 1, 0), (0, 3, 0))
 SPREAD = (
@@ -79,9 +83,9 @@
         return first
 
 
-N_SEND = 48
-N_RECV = 112
-N_LOCAL = 32
+N_SEND = 35
+N_RECV = 96
+N_LOCAL = 17
 
 
 def kernel(*refs):
@@ -192,14 +196,15 @@
     def passes_on(core, block):
         return (c == core) & (block < flip(block, 2))
 
-    l_recv = {k: in_sem.take(len(GATHER[k])) for k in (1, 2, 3)}
+    l_recv = {k: in_sem.take(len(GATHER[k][0])) for k in (1, 2, 3)}
     l_fwd = {k: in_sem.take() for k in (1, 2, 3)}
-    l_send = {k: out_sem.take(len(GATHER[k])) for k in (1, 2, 3)}
+    l_send = {k: out_sem.take(len(GATHER[k][0])) for k in (1, 2, 3)}
     l_fsend = {k: out_sem.take() for k in (1, 2, 3)}
 
     def l_bulk(k, step):
         ref = lbuf[k]
-        count = len(STAGE[GATHER[k][step]]) * len(held_before(GATHER[k], step))
+        order = GATHER[k][0]
+        count = len(STAGE[order[step]]) * len(held_before(order, step))
         if count == 3:
             return ref.at[0, 0, 0:3, 0]
         if count == 4:
@@ -216,14 +221,25 @@
     def l_source(k, mask):
         return loads[k] if mask == (0, 0, 0) else l_at(k, mask, c)
 
+    def by_order(k, step, run):
+        zero, one = GATHER[k]
+        if zero[:step + 1] == one[:step + 1]:
+            run(zero)
+        else:
+            pl.when(c == 0)(lambda: run(zero))
+            pl.when(c == 1)(lambda: run(one))
+
     def l_step(k, step, cond=None):
+        def stage_of(order):
+            for mask in STAGE[order[step]]:
+                for held in held_before(order, step):
+                    send(l_source(k, held), l_at(k, held, c), l_send[k] + step, l_recv[k] + step,
+                         dev(mask))
+
         def run():
             if step > 0:
                 l_collect(k, step - 1)
-            for mask in STAGE[GATHER[k][step]]:
-                for held in held_before(GATHER[k], step):
-                    send(l_source(k, held), l_at(k, held, c), l_send[k] + step, l_recv[k] + step,
-                         dev(mask))
+            by_order(k, step, stage_of)
 
         if cond is None:
             run()
@@ -235,10 +251,14 @@
 
     def l_collect(k, step):
         wait_recv(l_bulk(k, step), l_recv[k] + step)
-        for mask in STAGE[GATHER[k][step]]:
-            for held in held_before(GATHER[k], step):
-                ref = l_at(k, xor(held, mask), c)
-                send(ref, ref, l_fsend[k], l_fwd[k], sib)
+
+        def forward(order):
+            for mask in STAGE[order[step]]:
+                for held in held_before(order, step):
+                    ref = l_at(k, xor(held, mask), c)
+                    send(ref, ref, l_fsend[k], l_fwd[k], sib)
+
+        by_order(k, step, forward)
 
     l_own = {}
     l_done = set()
@@ -491,7 +511,7 @@
                 l_step(2, 2)
                 l_step(3, 2)
             else:
-                l_collect(k + 1, len(GATHER[k + 1]) - 1)
+                l_collect(k + 1, len(GATHER[k + 1][0]) - 1)
             l_finish(k + 1)
             l_product(k + 1)
         return run
@@ -521,8 +541,7 @@
             pl.when(cond)(lambda src=src, si=si: wait_send(src, si))
     for copy in out_copies:
         copy.wait()
-    used = (out_sem.used, in_sem.used, local.used)
-    assert used <= (N_SEND, N_RECV, N_LOCAL) and max(used) <= N_RECV, used
+    assert (out_sem.used, in_sem.used, local.used) == (N_SEND, N_RECV, N_LOCAL)
 
 
 def hand_over(*refs):

time: 116 us -> 120 us (1.034)
  Pallas kernels: 115 us -> 119 us
    pallas_call x1, Pallas kernels: 114 us -> 117 us  [per_device(): pl.pallas_call(kernel, out_shape=shapes, in_specs=[anywhere] * 12 + [pl.B...]
where the time goes in v5:
time: 120 us; the launch traced here: 119 us
  Pallas kernels  119 us (99%)
    pallas_call x1, Pallas kernels, per_device(): pl.pallas_call(kernel, out_shape=shapes, in_specs=[anywhere] * 12 + [pl.B...  117 us

profile of v5, /device:TPU:1, one launch (start us, length us, event | category | flops | bytes accessed | tf_op | source)
XLA Modules:
  0.0 119.4 jit_solution(236915111147247698)
XLA Ops:
  0.6 116.7 %shard_map.182 = (bf16[768,256]{1,0:T(8,128)(2,1)}, bf16[384,256]{1,0:T(8,128)(2,1)}, bf16[192,256]{1,0:T(8,128)(2,1)}, bf16[96,256]{1,0:T(8,128)(2,1)}, f32[24,256]{1,0:T(8,128)}) custom-call(bf16[768,256]{1,0:T(8,128)(2,1)} %refs_0_.1, bf16[384,256]{1,0:T(8,128)(2,1)} %refs_1_.1, bf16[192,256]{1,0:T(8,128)(2,1)} %refs_2_.1, bf16[96,256]{1,0:T(8,128)(2,1)} %refs_3_.1, ...), custom_call_target="tpu_custom_call" | custom-call | tf_op jit(solution)/shard_map/pallas_call | solution.py:585
  117.3 1.9 %shard_map.183 = (bf16[768,256]{1,0:T(8,128)(2,1)}, bf16[384,256]{1,0:T(8,128)(2,1)}, bf16[192,256]{1,0:T(8,128)(2,1)}, bf16[96,256]{1,0:T(8,128)(2,1)}, f32[24,256]{1,0:T(8,128)}) custom-call(bf16[768,256]{1,0:T(8,128)(2,1)} %get-tuple-element.10.refs_0_, bf16[384,256]{1,0:T(8,128)(2,1)} %get-tuple-element.11.refs_1_, ...), custom_call_target="tpu_custom_call" | custom-call | tf_op jit(solution)/shard_map/pallas_call | solution.py:595

commit v6 on v4

--- a/solution.py
+++ b/solution.py
@@ -41,7 +41,7 @@
 NZ = {1: 2, 2: 4, 3: 4}
 NCH = 3
 PCH = 4
-PARTS = (2, 2, 2, 1)
+PARTS = (4, 2, 2, 1)
 
 
 def flip(value, mask):
@@ -79,9 +79,9 @@
         return first
 
 
-N_SEND = 48
-N_RECV = 112
-N_LOCAL = 32
+N_SEND = 35
+N_RECV = 110
+N_LOCAL = 17
 
 
 def kernel(*refs):
@@ -521,8 +521,7 @@
             pl.when(cond)(lambda src=src, si=si: wait_send(src, si))
     for copy in out_copies:
         copy.wait()
-    used = (out_sem.used, in_sem.used, local.used)
-    assert used <= (N_SEND, N_RECV, N_LOCAL) and max(used) <= N_RECV, used
+    assert (out_sem.used, in_sem.used, local.used) == (N_SEND, N_RECV, N_LOCAL)
 
 
 def hand_over(*refs):

time: 116 us -> 117 us (level)
  no operation moved by 1% of the time
where the time goes in v6:
time: 117 us
  Pallas kernels  116 us (99%)
    pallas_call x1, Pallas kernels, per_device(): pl.pallas_call(kernel, out_shape=shapes, in_specs=[anywhere] * 12 + [pl.B...  114 us

profile of v6, /device:TPU:1, one launch (start us, length us, event | category | flops | bytes accessed | tf_op | source)
XLA Modules:
  0.0 116.6 jit_solution(16634686825224886905)
XLA Ops:
  0.6 113.8 %shard_map.182 = (bf16[768,256]{1,0:T(8,128)(2,1)}, bf16[384,256]{1,0:T(8,128)(2,1)}, bf16[192,256]{1,0:T(8,128)(2,1)}, bf16[96,256]{1,0:T(8,128)(2,1)}, f32[24,256]{1,0:T(8,128)}) custom-call(bf16[768,256]{1,0:T(8,128)(2,1)} %refs_0_.1, bf16[384,256]{1,0:T(8,128)(2,1)} %refs_1_.1, bf16[192,256]{1,0:T(8,128)(2,1)} %refs_2_.1, bf16[96,256]{1,0:T(8,128)(2,1)} %refs_3_.1, ...), custom_call_target="tpu_custom_call" | custom-call | tf_op jit(solution)/shard_map/pallas_call | solution.py:565
  114.5 1.9 %shard_map.183 = (bf16[768,256]{1,0:T(8,128)(2,1)}, bf16[384,256]{1,0:T(8,128)(2,1)}, bf16[192,256]{1,0:T(8,128)(2,1)}, bf16[96,256]{1,0:T(8,128)(2,1)}, f32[24,256]{1,0:T(8,128)}) custom-call(bf16[768,256]{1,0:T(8,128)(2,1)} %get-tuple-element.10.refs_0_, bf16[384,256]{1,0:T(8,128)(2,1)} %get-tuple-element.11.refs_1_, ...), custom_call_target="tpu_custom_call" | custom-call | tf_op jit(solution)/shard_map/pallas_call | solution.py:575
